TPU v7x, 32 devices: a whole 2x2x4 slice. The times are simulated.
32 devices in a mesh: cp: 32 (over z, y, x, core).
Axes of the slice: x: 2, y: 2, z: 4, core: 2. Of those that a mesh axis runs over, the one named last changes fastest.
Arguments:
- u_in: bfloat16 [16, 2048, 5376], P(None, 'cp')
- seg_ids: int32 [16, 2048], P(None, 'cp')
- grad_h: float32 [16, 2048, 5376], P(None, 'cp')
- conv_w: float32 [4, 5376], replicated
- conv_b: float32 [5376], replicated
- a_gate_w: bfloat16 [21, 256, 256], replicated
- a_gate_b: float32 [5376], replicated
- x_gate_w: bfloat16 [21, 256, 256], replicated
- x_gate_b: float32 [5376], replicated
- lam_param: float32 [5376], replicated
Outputs:
- output 1: bfloat16 [16, 2048, 5376], P(None, 'cp')
- output 2: float32 [4, 5376], replicated
- output 3: float32 [5376], replicated
- output 4: float32 [21, 256, 256], replicated
- output 5: float32 [5376], replicated
- output 6: float32 [21, 256, 256], replicated
- output 7: float32 [5376], replicated
- output 8: float32 [5376], replicated
All inputs are finite; a program needn't handle non-finite values.
Results may differ from a plain program's by a relative error of at most 0.001.
Values sent between devices are 32-bit elements.
A program may use at most 1 GiB of HBM per device.

v0:
```python
import jax
import jax.numpy as jnp
from jax import lax
from jax.sharding import PartitionSpec as P

CONV = 4


def solution(mesh):
    n_dev = mesh.shape['cp']
    to_next = [(src, src + 1) for src in range(n_dev - 1)]
    to_prev = [(src + 1, src) for src in range(n_dev - 1)]
    seq_spec = P(None, 'cp', None)
    rep_spec = P()

    def local_fn(u_in, seg_ids, grad_h, conv_w, conv_b, a_gate_w, a_gate_b, x_gate_w, x_gate_b, lam_param):
        n_batch, n_tok, n_width = u_in.shape
        n_heads, block_w, _ = a_gate_w.shape
        n_halo = CONV - 1
        has_prev = lax.axis_index('cp') > 0
        tail_pack = jnp.concatenate([u_in[:, n_tok - n_halo:, :].astype(jnp.float32),
                                     seg_ids[:, n_tok - n_halo:, None].astype(jnp.float32)], axis=2)
        recv_pack = lax.ppermute(tail_pack, 'cp', to_next)
        tail_u = recv_pack[:, :, :n_width].astype(jnp.bfloat16)
        tail_seg = recv_pack[:, :, n_width].astype(jnp.int32)
        u_ext = jnp.swapaxes(jnp.concatenate([tail_u, u_in], axis=1), 0, 1)
        seg_ext = jnp.concatenate([tail_seg, seg_ids], axis=1).T
        ext_ok = (jnp.arange(n_tok + n_halo) >= n_halo) | has_prev
        seg_here = seg_ext[n_halo:]
        mask_list = []
        u_list = []
        conv_out = conv_b
        for offset in range(CONV):
            start_at = n_halo - offset
            seg_shift = seg_ext[start_at:start_at + n_tok]
            tap_ok = (seg_shift == seg_here) & ext_ok[start_at:start_at + n_tok, None]
            tap_mask = tap_ok[:, :, None].astype(jnp.float32)
            u_shift = u_ext[start_at:start_at + n_tok]
            mask_list.append(tap_mask)
            u_list.append(u_shift)
            conv_out = conv_out + conv_w[offset] * tap_mask * u_shift
        reset = mask_list[1] < 0.5
        conv_bf = conv_out.astype(jnp.bfloat16).reshape(n_tok, n_batch, n_heads, block_w)
        pre_a = jnp.einsum('lbhk,hkj->lbhj', conv_bf, a_gate_w, preferred_element_type=jnp.float32).reshape(n_tok, n_batch, n_width) + a_gate_b
        pre_i = jnp.einsum('lbhk,hkj->lbhj', conv_bf, x_gate_w, preferred_element_type=jnp.float32).reshape(n_tok, n_batch, n_width) + x_gate_b
        gate_r = jax.nn.sigmoid(pre_a)
        gate_i = jax.nn.sigmoid(pre_i)
        soft_lam = jax.nn.softplus(-lam_param)
        log_a = -8.0 * gate_r * soft_lam
        decay_a = jnp.where(reset, 0.0, jnp.exp(log_a))
        root_mult = jnp.sqrt(-jnp.expm1(2.0 * log_a))
        multiplier = jnp.where(reset, 1.0, root_mult)
        x_t = multiplier * gate_i * conv_out
        grad_tm = jnp.swapaxes(grad_h, 0, 1)
        zero_state = jnp.zeros((n_batch, n_width), jnp.float32)
        one_state = jnp.ones((n_batch, n_width), jnp.float32)

        def fwd_step(carry_in, step_in):
            run_state, run_prod = carry_in
            dec_t, inp_t = step_in
            run_state = dec_t * run_state + inp_t
            run_prod = dec_t * run_prod
            return (run_state, run_prod), (run_state, run_prod)

        (end_state, end_prod), (h_local, prod_upto) = lax.scan(fwd_step, (zero_state, one_state), (decay_a, x_t))

        def bwd_step(carry_in, step_in):
            adj_next, run_prod = carry_in
            dec_t, grad_t = step_in
            adj_t = grad_t + adj_next
            return (dec_t * adj_t, dec_t * run_prod), (adj_t, run_prod)

        (first_term, _), (adj_local, prod_after) = lax.scan(bwd_step, (zero_state, one_state), (decay_a, grad_tm), reverse=True)

        def fwd_chain(_, state_cur):
            return lax.ppermute(end_prod * state_cur + end_state, 'cp', to_next)

        state_in = lax.fori_loop(0, n_dev - 1, fwd_chain, zero_state)

        def bwd_chain(_, adj_cur):
            return lax.ppermute(end_prod * adj_cur + first_term, 'cp', to_prev)

        adj_in = lax.fori_loop(0, n_dev - 1, bwd_chain, zero_state)
        hidden = h_local + prod_upto * state_in
        h_prev = jnp.concatenate([state_in[None], hidden[:-1]], axis=0)
        adjoint = adj_local + prod_after * adj_in
        d_mult = adjoint * gate_i * conv_out
        d_log = adjoint * h_prev * decay_a - d_mult * decay_a * decay_a / root_mult
        d_conv = adjoint * multiplier * gate_i
        d_pre_a = d_log * (-8.0 * soft_lam) * gate_r * (1.0 - gate_r)
        d_pre_i = adjoint * multiplier * conv_out * gate_i * (1.0 - gate_i)
        g_lam = 8.0 * jax.nn.sigmoid(-lam_param) * jnp.sum(d_log * gate_r, axis=(0, 1))
        ga_bf = d_pre_a.astype(jnp.bfloat16).reshape(n_tok, n_batch, n_heads, block_w)
        gi_bf = d_pre_i.astype(jnp.bfloat16).reshape(n_tok, n_batch, n_heads, block_w)
        back_a = jnp.einsum('lbhj,hkj->lbhk', ga_bf, a_gate_w, preferred_element_type=jnp.float32)
        back_i = jnp.einsum('lbhj,hkj->lbhk', gi_bf, x_gate_w, preferred_element_type=jnp.float32)
        d_conv = d_conv + (back_a + back_i).reshape(n_tok, n_batch, n_width)
        g_wa = jnp.einsum('lbhk,lbhj->hkj', conv_bf, ga_bf, preferred_element_type=jnp.float32)
        g_wi = jnp.einsum('lbhk,lbhj->hkj', conv_bf, gi_bf, preferred_element_type=jnp.float32)
        du_ext = jnp.zeros((n_tok + n_halo, n_batch, n_width), jnp.float32)
        g_w_list = []
        for offset in range(CONV):
            masked = mask_list[offset] * d_conv
            du_ext = du_ext + jnp.pad(conv_w[offset] * masked, ((n_halo - offset, offset), (0, 0), (0, 0)))
            g_w_list.append(jnp.sum(masked * u_list[offset], axis=(0, 1)))
        halo_back = lax.ppermute(du_ext[:n_halo], 'cp', to_prev)
        du_local = du_ext[n_halo:] + jnp.pad(halo_back, ((n_tok - n_halo, 0), (0, 0), (0, 0)))
        grad_u = jnp.swapaxes(du_local.astype(jnp.bfloat16), 0, 1)
        totals = lax.psum((jnp.stack(g_w_list), jnp.sum(d_conv, axis=(0, 1)), g_wa, jnp.sum(d_pre_a, axis=(0, 1)),
                           g_wi, jnp.sum(d_pre_i, axis=(0, 1)), g_lam), 'cp')
        return (grad_u,) + tuple(totals)

    return jax.shard_map(local_fn, mesh=mesh,
                         in_specs=(seq_spec, P(None, 'cp'), seq_spec, rep_spec, rep_spec, rep_spec,
                                   rep_spec, rep_spec, rep_spec, rep_spec),
                         out_specs=(seq_spec,) + (rep_spec,) * 7, check_vma=False)
```

profile of v0, /device:TPU:0, one launch (start us, length us, event | category | flops | bytes accessed | tf_op | source)
XLA Modules:
  0.0 2162.0 jit_solution(12929361443308831851)
XLA Ops:
  7.2 13.3 copy.86
  26.4 22.3 %copy.160 = f32[16,64,5376]{2,0,1:T(8,128)} copy(f32[16,64,5376]{2,1,0:T(8,128)} %param.20) | data formatting | bytes 44040192 | tf_op args[2]
  62.8 31.4 %fusion.65 = (bf16[64,16,5376]{2,1,0:T(8,128)(2,1)}, f32[64,16,5376]{2,1,0:T(8,128)}) fusion(bf16[67,16,5376]{2,1,0:T(8,128)(2,1)} %maximum_bitcast_fusion, f32[64,16]{1,0:T(8,128)S(1)} %copy.94, f32[5376]{0:T(1024)} %get-tuple-element.339, f32[64,16]{1,0:T(8,128)S(1)} %copy.93, f32[5376]{0:T(1024)} %get-tuple-element.340, f32[64,16]{1,0:T(8,128)S(1)} %copy.92, ...), kind=kLoop, calls=%fused_computation.114 | loop fusion | flops 93585408 | bytes 77190400 | tf_op jit(solution)/shard_map/convert_element_type | solution.py:43
  94.2 18.7 reshape.66
  112.9 15.2 fusion.31
  128.1 16.3 copy.117
  144.4 14.5 fusion.34
  158.9 16.0 copy.118
  175.0 44.2 %multiply_multiply_fusion.1 = (f32[64,16,5376]{2,1,0:T(8,128)}, f32[64,16,5376]{2,1,0:T(8,128)}) fusion(f32[64,16,5376]{2,1,0:T(8,128)} %get-tuple-element.401, pred[64,16]{1,0:T(8,128)(4,1)S(1)} %copy.90, f32[5376]{0:T(1024)S(1)} %copy-done.12, f32[64,16,5376]{2,1,0:T(8,128)} %bitcast.97, f32[5376]{0:T(1024)S(1)} %copy-done.11, ...), kind=kLoop, calls=%fused_computation.43 | loop fusion | flops 82575360 | bytes 110166016 | tf_op jit(solution)/shard_map/mul | solution.py:53
  219.3 10.1 broadcast.48.clone
  239.3 140.3 %while.61 = (s32[]{:T(128)}, f32[16,5376]{1,0:T(8,128)S(1)}, f32[16,5376]{1,0:T(8,128)S(1)}, f32[64,16,5376]{2,1,0:T(8,128)}, f32[64,16,5376]{2,1,0:T(8,128)}, /...) while((s32[]{:T(128)}, f32[16,5376]{1,0:T(8,128)S(1)}, ...), condition=%wide.region_3.4_spmd.clone, body=%wide.region_2.3_spmd.clone.sunk | while | flops 430083 | bytes 2752627 | solution.py:65
  390.4 10.1 broadcast.48.clone.3
  400.5 263.1 %while.60 = (s32[]{:T(128)}, f32[16,5376]{1,0:T(8,128)S(1)}, f32[16,5376]{1,0:T(8,128)}, f32[64,16,5376]{2,1,0:T(8,128)}, f32[64,16,5376]{2,1,0:T(8,128)}, /*ind...) while((s32[]{:T(128)}, f32[16,5376]{1,0:T(8,128)S(1)}, ...), condition=%wide.region_1.2_spmd.clone, body=%wide.region_0.1_spmd.clone.sunk | while | flops 688132 | bytes 3784844 | solution.py:73
  664.4 339.4 %while.59 = (s32[]{:T(128)}, f32[16,5376]{1,0:T(8,128)}, f32[16,5376]{1,0:T(8,128)S(1)}, f32[16,5376]{1,0:T(8,128)}, s32[]{:T(128)}) while((s32[]{:T(128)}, f32[16,5376]{1,0:T(8,128)}, f32[16,5376]{1,0:T(8,128)S(1)}, f32[16,5376]{1,0:T(8,128)}, s32[]{:T(128)}) %tuple.149), condition=%wide.region_7.8_spmd, body=%wide.region_6.7_spmd.sunk | while | flops 172034 | bytes 2752613 | solution.py:78
  1003.7 22.3 %slice_add_fusion.1 = f32[63,16,5376]{2,1,0:T(8,128)} fusion(f32[64,16,5376]{2,1,0:T(8,128)} %get-tuple-element.242, f32[64,16,5376]{2,1,0:T(8,128)} %get-tuple-element.243, f32[16,5376]{1,0:T(8,128)} %get-tuple-element.241), kind=kLoop, calls=%fused_computation.48 | loop fusion | flops 10838016 | bytes 65372160 | tf_op jit(solution)/shard_map/add | solution.py:84
  1026.9 378.0 %while.58 = (s32[]{:T(128)}, f32[16,5376]{1,0:T(8,128)}, f32[16,5376]{1,0:T(8,128)S(1)}, f32[16,5376]{1,0:T(8,128)S(1)}, s32[]{:T(128)}) while((s32[]{:T(128)}, f32[16,5376]{1,0:T(8,128)}, f32[16,5376]{1,0:T(8,128)S(1)}, f32[16,5376]{1,0:T(8,128)S(1)}, s32[]{:T(128)}) %tuple.148), condition=%wide.region_5.6_spmd, body=%wide.region_4.5_spmd.sunk | while | flops 172034 | bytes 2752613 | solution.py:83
  1404.8 64.0 %multiply_reduce_fusion = (f32[5376]{0:T(1024)}, f32[5376]{0:T(1024)}, f32[64,16,5376]{2,1,0:T(8,128)}, f32[5376]{0:T(1024)}, f32[64,16,5376]{2,1,0:T(8,128)}) fusion(f32[64,16,5376]{2,1,0:T(8,128)} %bitcast.102, f32[5376]{0:T(1024)S(1)} %copy-done.17, f32[5376]{0:T(1024)S(1)} %copy-done.12, f32[64,16,5376]{2,1,0:T(8,128)} %get-tuple-element.401, ...), kind=kLoop, calls=%fused_computation.37 | loop fusion | flops 203669760 | bytes 176634880 | tf_op jit(solution)/shard_map/reduce_sum | solution.py:92
  1468.8 43.8 %fusion.40 = (bf16[64,16,5376]{2,1,0:T(8,128)(2,1)}, bf16[64,16,5376]{2,1,0:T(8,128)(2,1)}) fusion(f32[64,16,5376]{2,1,0:T(8,128)} %get-tuple-element.398, f32[5376]{0:T(1024)S(1)} %copy-done.12, f32[64,16,5376]{2,1,0:T(8,128)} %bitcast.103, f32[5376]{0:T(1024)S(1)} %copy-done.17, f32[64,16,5376]{2,1,0:T(8,128)} %bitcast.99, f32[5376]{0:T(1024)S(1)} %copy-done.11, ...), kind=kLoop, calls=%fused_computation.78 | loop fusion | flops 99090432 | bytes 132185088 | tf_op jit(solution)/shard_map/convert_element_type | solution.py:93
  1512.6 18.6 reshape.70
  1531.3 11.5 fusion.13
  1542.8 18.8 reshape.69
  1561.6 19.9 add_bitcast_fusion
  1581.5 16.0 copy.119
  1597.6 45.3 %fusion.4 = (f32[5376]{0:T(1024)S(1)}, f32[5376]{0:T(1024)S(1)}, f32[5376]{0:T(1024)S(1)}, f32[5376]{0:T(1024)S(1)}, f32[5376]{0:T(1024)}, /*index=5*/f32[64,16,5376]{2,1,0:T(8,128)}) fusion(f32[64]{0:T(128)S(1)} %copy-done.26, bf16[67,16,5376]{2,1,0:T(8,128)(2,1)} %maximum_bitcast_fusion, f32[64,16]{1,0:T(8,128)S(1)} %copy-done.6, ...), kind=kLoop, calls=%fused_computation.26 | loop fusion | flops 126588672 | bytes 132262144 | tf_op jit(solution)/shard_map/reduce_sum | solution.py:105
  1643.0 45.6 %fusion.45 = f32[21,256,256]{2,1,0:T(8,128)} fusion(bf16[64,16,21,256]{3,2,1,0:T(8,128)(2,1)} %reshape.69, bf16[64,16,21,256]{3,2,1,0:T(8,128)(2,1)} %reshape.66), kind=kOutput, calls=%fused_computation.83 | convolution fusion | flops 2818572288 | bytes 27525120 | tf_op jit(solution)/shard_map/lbhk,lbhj->hkj/dot_general | solution.py:98
  1688.7 59.1 %fusion.50 = f32[21,256,256]{2,1,0:T(8,128)} fusion(bf16[64,16,21,256]{3,2,1,0:T(8,128)(2,1)} %reshape.70, bf16[64,16,21,256]{3,2,1,0:T(8,128)(2,1)} %reshape.66), kind=kOutput, calls=%fused_computation.84 | convolution fusion | flops 2818572288 | bytes 27525120 | tf_op jit(solution)/shard_map/lbhk,lbhj->hkj/dot_general | solution.py:99
  1749.2 36.0 %multiply_multiply_fusion.5 = (f32[64,16,5376]{2,1,0:T(8,128)}, f32[64,16,5376]{2,1,0:T(8,128)}, f32[64,16,5376]{2,1,0:T(8,128)}, f32[64,16,5376]{2,1,0:T(8,128)}) fusion(f32[64,16,5376]{2,1,0:T(8,128)} %get-tuple-element.399, f32[64]{0:T(128)S(1)} %copy-done.26, f32[5376]{0:T(1024)S(1)} %copy-done.13, f32[64,16]{1,0:T(8,128)S(1)} %copy-done.10, ...), kind=kLoop, calls=%fused_computation.53 | loop fusion | flops 44040192 | bytes 110199040 | tf_op jit(solution)/shard_map/mul | solution.py:104
  1788.1 36.1 %pad_add_fusion = f32[67,16,5376]{2,1,0:T(8,128)} fusion(f32[64,16,5376]{2,1,0:T(8,128)} %get-tuple-element.415, f32[64,16,5376]{2,1,0:T(8,128)} %get-tuple-element.416, f32[64,16,5376]{2,1,0:T(8,128)} %get-tuple-element.417, f32[64,16,5376]{2,1,0:T(8,128)} %get-tuple-element.414), kind=kLoop, calls=%fused_computation.21 | loop fusion | flops 17289216 | bytes 111132672 | tf_op jit(solution)/shard_map/add | solution.py:104
  1824.3 10.3 fusion.12
  1834.6 10.4 copy.107
  1845.0 68.7 %all-reduce.10.cloned.1.call-done = (f32[5376]{0:T(1024)}, f32[5376]{0:T(1024)}, f32[5376]{0:T(1024)}, f32[5376]{0:T(1024)}) async-done(((f32[5376]{0:T(1024)}, f32[5376]{0:T(1024)}, f32[5376]{0:T(1024)}, f32[5376]{0:T(1024)}), (f32[5376]{0:T(1024)}, f32[5376]{0:T(1024)}, f32[5376]{0:T(1024)}, f32[5376]{0:T(1024)})) %all-reduce.10.cloned.1.call-update) | async-done | bytes 86032 | tf_op jit(solution)/shard_map/psum | solution.py:109
  1913.7 224.5 %all-reduce.12.cloned.1.call-done = (f32[4,5376]{1,0:T(4,128)}, f32[21,256,256]{2,1,0:T(8,128)}, f32[21,256,256]{2,1,0:T(8,128)}) async-done(((f32[4,5376]{1,0:T(4,128)}, f32[21,256,256]{2,1,0:T(8,128)}, f32[21,256,256]{2,1,0:T(8,128)}), (f32[4,5376]{1,0:T(4,128)}, f32[21,256,256]{2,1,0:T(8,128)}, f32[21,256,256]{2,1,0:T(8,128)})) %all-reduce.12.cloned.1.call-update) | async-done | bytes 11096080 | tf_op jit(solution)/shard_map/psum | solution.py:109
  (481 shorter events, 1183.3 us)
Async XLA Ops:
  7.2 1906.5 %all-reduce.10.cloned.1.call-start = ((), (), s32[]{:S(2)}) async-start(), calls=%async_computation | async-start | bytes 196608 | tf_op jit(solution)/shard_map/psum | solution.py:109
  22.9 27.3 %collective-permute-start.2 = (f32[16,3,5377]{2,0,1:T(8,128)}, f32[16,3,5377]{2,0,1:T(8,128)}, u32[]{:S(2)}, u32[]{:S(2)}) collective-permute-start(f32[16,3,5377]{2,0,1:T(8,128)} %pad_maximum_fusion), channel_id=1, source_target_pairs={{0,1},{1,2},{2,3},{3,4},{4,5},{5,6},{6,7},{7,8},{8,9},{9,10},{10,1... | collective-permute-start | bytes 3097160 | tf_op jit(solution)/shard_map/ppermute | solution.py:23
  944.5 10.4 collective-permute-start.1
  956.7 10.4 collective-permute-start.1
  968.9 10.4 collective-permute-start.1
  981.2 10.4 collective-permute-start.1
  993.4 10.4 collective-permute-start.1
  1040.6 11.1 collective-permute-start
  1065.4 11.1 collective-permute-start
  1090.2 11.1 collective-permute-start
  1115.0 11.1 collective-permute-start
  1127.9 10.4 collective-permute-start
  1140.0 10.4 collective-permute-start
  1152.2 10.4 collective-permute-start
  1164.3 10.4 collective-permute-start
  1188.5 10.4 collective-permute-start
  1200.6 10.4 collective-permute-start
  1212.7 10.4 collective-permute-start
  1237.0 10.4 collective-permute-start
  1249.1 10.4 collective-permute-start
  1261.2 10.4 collective-permute-start
  1273.3 10.4 collective-permute-start
  1297.5 10.4 collective-permute-start
  1309.7 10.4 collective-permute-start
  1321.8 10.4 collective-permute-start
  1333.9 10.4 collective-permute-start
  1358.1 10.4 collective-permute-start
  1370.2 10.4 collective-permute-start
  1382.4 10.4 collective-permute-start
  1394.5 10.4 collective-permute-start
  1748.4 389.8 %all-reduce.12.cloned.1.call-start = ((), (), s32[]{:S(2)}) async-start(), calls=%async_computation.1 | async-start | bytes 22192128 | tf_op jit(solution)/shard_map/psum | solution.py:109
  1786.8 37.4 %collective-permute-start.3 = (f32[3,16,5376]{2,1,0:T(8,128)S(1)}, f32[3,16,5376]{2,1,0:T(8,128)S(1)}, u32[]{:S(2)}, u32[]{:S(2)}) collective-permute-start(f32[3,16,5376]{2,1,0:T(8,128)S(1)} %pad_add_fusion.1), channel_id=1, source_target_pairs={{1,0},{2,1},{3,2},{4,3},{5,4},{6,5},{7,6},{8,7},{9,8},{10,9},{11,1... | collective-permute-start | bytes 3096584 | tf_op jit(solution)/shard_map/ppermute | solution.py:106
  (61 other events, 1970.8 us)
Sparse Core Ops, SparseCore 0:
  1748.5 165.1 all-reduce.9
  1920.7 217.4 all-reduce.11
where the time goes:
time: 2180 us; the launch traced here: 2160 us
  other arithmetic  865 us (40%)
  waiting for transfers between devices  593 us (27%)
  starting transfers between devices  310 us (14%)
  local copies, waits for them, and re-layouts  213 us (10%)
  matrix products  166 us (8%)
    psum x2, waiting for transfers between devices, local_fn(): lax.psum((jnp.stack(g_w_list), jnp.sum(d_conv, axis=(0, 1)), g_wa, jnp.su...  293 us
    ppermute x31, waiting for transfers between devices, bwd_chain(): return lax.ppermute(end_prod * adj_cur + first_term, 'cp', to_prev)  283 us
    dynamic_update_slice x128, other arithmetic, local_fn(): lax.scan(fwd_step, (zero_state, one_state), (decay_a, x_t))  268 us
    ppermute x31, starting transfers between devices, fwd_chain(): return lax.ppermute(end_prod * state_cur + end_state, 'cp', to_next)  265 us
    mul x64, other arithmetic, bwd_step(): return ((dec_t * adj_t, dec_t * run_prod), (adj_t, run_prod))  134 us
    reduce_sum x1, other arithmetic, local_fn(): jnp.sum(d_log * gate_r, axis=(0, 1))  64 us
    unnamed x65, local copies, waits for them, and re-layouts  63.5 us
    dot_general x1, matrix products, local_fn(): jnp.einsum('lbhk,lbhj->hkj', conv_bf, gi_bf, preferred_element_type=jnp.f...  59.1 us
  transfers between devices with their start and end apart: 66, of which 64 were waited for; matrix products, arithmetic and copies ran while one was open for 6% of the time, Pallas kernels for 0%

commit v1 on v0

v1 whole, which is shorter than its diff:
```python
import functools

import jax
import jax.numpy as jnp
from jax import lax
from jax.experimental import pallas as pl
from jax.experimental.pallas import tpu as pltpu
from jax.sharding import PartitionSpec as P

CONV = 4
HALO = CONV - 1
LOG2E = 1.4426950408889634
LANES = 128
STEPS = 8

W0, BC, BA, BI, KL, KE = 0, 4, 5, 6, 7, 8
N_PAR = 16
GW, GBC, GBA, GBI, GLAM = 0, 4, 5, 6, 7
N_VEC = 8


def sigmoid_of(pre):
    root = lax.rsqrt(1.0 + jnp.exp2(pre * (-LOG2E)))
    return root * root


def decay_of(gate_r, par_kl, par_ke, keep):
    a_raw = jnp.exp2(gate_r * par_ke)
    gap = jnp.tanh(gate_r * (-par_kl)) * (1.0 + a_raw * a_raw)
    inv_root = lax.rsqrt(gap)
    decay = a_raw * keep
    mult = jnp.where(keep > 0.5, gap * inv_root, 1.0)
    return decay, mult, decay * decay * inv_root


def fold_rows(arr):
    return arr[:8] + arr[8:]


def dot_nn(lhs, rhs):
    return lax.dot_general(lhs, rhs, (((1,), (0,)), ((), ())), preferred_element_type=jnp.float32)


def dot_nt(lhs, rhs):
    return lax.dot_general(lhs, rhs, (((1,), (1,)), ((), ())), preferred_element_type=jnp.float32)


def dot_tn(lhs, rhs):
    return lax.dot_general(lhs, rhs, (((0,), (0,)), ((), ())), preferred_element_type=jnp.float32)


def load_u(u_ref, halo_ref, u_scr):
    n_tok = u_ref.shape[1]
    u_scr[:HALO] = halo_ref[...]
    for start in range(0, n_tok, 16):
        u_scr[HALO + start:HALO + start + 16] = jnp.swapaxes(u_ref[:, start:start + 16, :].astype(jnp.float32), 0, 1)


def first_kernel(u_ref, gh_ref, halo_ref, mask_ref, wa_ref, wi_ref, par_ref,
                 sum_ref, c_ref, r_ref, i_ref, u_scr, cb_scr, pa_scr, pi_scr, a_scr, g_scr):
    n_batch, n_tok, width = u_ref.shape
    load_u(u_ref, halo_ref, u_scr)

    def conv_body(chunk, _):
        base = chunk * STEPS
        for step in range(STEPS):
            tok = base + step
            for lane in range(0, width, LANES):
                cols = slice(lane, lane + LANES)
                acc = par_ref[BC:BC + 1, cols] + par_ref[W0:W0 + 1, cols] * u_scr[tok + HALO, :, cols]
                for tap in range(1, CONV):
                    acc = acc + par_ref[W0 + tap:W0 + tap + 1, cols] * (mask_ref[tap - 1, tok] * u_scr[tok + HALO - tap, :, cols])
                c_ref[tok, :, cols] = acc
                cb_scr[tok, :, cols] = acc.astype(jnp.bfloat16)
        return 0

    lax.fori_loop(0, n_tok // STEPS, conv_body, 0)
    rows = 256
    for start in range(0, n_tok, rows // n_batch):
        toks = slice(start, start + rows // n_batch)
        part = cb_scr[toks].reshape(rows, width)
        pa_scr[toks] = dot_nn(part, wa_ref[0]).reshape(rows // n_batch, n_batch, width)
        pi_scr[toks] = dot_nn(part, wi_ref[0]).reshape(rows // n_batch, n_batch, width)

    for start in range(0, n_tok, 8):
        g_scr[start:start + 8] = jnp.swapaxes(gh_ref[:, start:start + 8, :], 0, 1)

    for lane in range(0, width, LANES):
        cols = slice(lane, lane + LANES)

        def fwd_body(chunk, carry):
            state, prod = carry
            base = chunk * STEPS
            for step in range(STEPS):
                tok = base + step
                gate_r = sigmoid_of(pa_scr[tok, :, cols] + par_ref[BA:BA + 1, cols])
                gate_i = sigmoid_of(pi_scr[tok, :, cols] + par_ref[BI:BI + 1, cols])
                decay, mult, _ = decay_of(gate_r, par_ref[KL:KL + 1, cols], par_ref[KE:KE + 1, cols], mask_ref[0, tok])
                r_ref[tok, :, cols] = gate_r
                i_ref[tok, :, cols] = gate_i
                a_scr[tok, :, cols] = decay
                state = decay * state + mult * (gate_i * c_ref[tok, :, cols])
                prod = decay * prod
            return state, prod

        zero = jnp.zeros((n_batch, LANES), jnp.float32)
        state, prod = lax.fori_loop(0, n_tok // STEPS, fwd_body, (zero, zero + 1.0))
        sum_ref[0, :, cols] = prod
        sum_ref[1, :, cols] = state

        def bwd_body(chunk, adj):
            base = n_tok - STEPS - chunk * STEPS
            for step in reversed(range(STEPS)):
                tok = base + step
                adj = a_scr[tok, :, cols] * (g_scr[tok, :, cols] + adj)
            return adj

        sum_ref[2, :, cols] = lax.fori_loop(0, n_tok // STEPS, bwd_body, zero)


def second_kernel(u_ref, gh_ref, halo_ref, mask_ref, wa_ref, wi_ref, par_ref, c_ref, r_ref, i_ref, in_ref,
                  du_ref, tail_ref, back_ref, dwa_ref, dwi_ref, vec_ref,
                  u_scr, cb_scr, ga_scr, gi_scr, a_scr, m_scr, e_scr, h_scr, d_scr, g_scr):
    n_batch, n_tok, width = u_ref.shape
    load_u(u_ref, halo_ref, u_scr)
    for start in range(0, n_tok, 8):
        g_scr[start:start + 8] = jnp.swapaxes(gh_ref[:, start:start + 8, :], 0, 1)

    for lane in range(0, width, LANES):
        cols = slice(lane, lane + LANES)
        zero8 = jnp.zeros((8, LANES), jnp.float32)

        def fwd_body(chunk, state):
            base = chunk * STEPS
            for step in range(STEPS):
                tok = base + step
                conv_c = c_ref[tok, :, cols]
                decay, mult, ratio = decay_of(r_ref[tok, :, cols], par_ref[KL:KL + 1, cols], par_ref[KE:KE + 1, cols], mask_ref[0, tok])
                a_scr[tok, :, cols] = decay
                m_scr[tok, :, cols] = mult
                e_scr[tok, :, cols] = ratio
                h_scr[tok, :, cols] = state
                cb_scr[tok, :, cols] = conv_c.astype(jnp.bfloat16)
                state = decay * state + mult * (i_ref[tok, :, cols] * conv_c)
            return state

        lax.fori_loop(0, n_tok // STEPS, fwd_body, in_ref[0, :, cols])

        def bwd_body(chunk, carry):
            adj_next, sum_a, sum_i, sum_l = carry
            base = n_tok - STEPS - chunk * STEPS
            for step in reversed(range(STEPS)):
                tok = base + step
                gate_r = r_ref[tok, :, cols]
                gate_i = i_ref[tok, :, cols]
                conv_c = c_ref[tok, :, cols]
                adj = g_scr[tok, :, cols] + adj_next
                adj_next = a_scr[tok, :, cols] * adj
                d_log = adj_next * h_scr[tok, :, cols] - adj * (gate_i * conv_c) * e_scr[tok, :, cols]
                direct = adj * m_scr[tok, :, cols] * gate_i
                d_pre_i = direct * conv_c * (1.0 - gate_i)
                d_log_r = d_log * gate_r
                d_pre_a = d_log_r * (par_ref[KL:KL + 1, cols] * (1.0 - gate_r))
                sum_l = sum_l + fold_rows(d_log_r)
                sum_a = sum_a + fold_rows(d_pre_a)
                sum_i = sum_i + fold_rows(d_pre_i)
                d_scr[tok, :, cols] = direct
                ga_scr[tok, :, cols] = d_pre_a.astype(jnp.bfloat16)
                gi_scr[tok, :, cols] = d_pre_i.astype(jnp.bfloat16)
            return adj_next, sum_a, sum_i, sum_l

        _, sum_a, sum_i, sum_l = lax.fori_loop(0, n_tok // STEPS, bwd_body, (in_ref[1, :, cols], zero8, zero8, zero8))
        vec_ref[0, GBA:GBA + 1, cols] = jnp.sum(sum_a, axis=0, keepdims=True)
        vec_ref[0, GBI:GBI + 1, cols] = jnp.sum(sum_i, axis=0, keepdims=True)
        vec_ref[0, GLAM:GLAM + 1, cols] = jnp.sum(sum_l, axis=0, keepdims=True)

    rows = 256
    for start in range(0, n_tok, rows // n_batch):
        toks = slice(start, start + rows // n_batch)
        back = dot_nt(ga_scr[toks].reshape(rows, width), wa_ref[0]) + dot_nt(gi_scr[toks].reshape(rows, width), wi_ref[0])
        d_scr[toks] = d_scr[toks] + back.reshape(rows // n_batch, n_batch, width)
    all_c = cb_scr[...].reshape(n_tok * n_batch, width)
    dwa_ref[0] = dot_tn(all_c, ga_scr[...].reshape(n_tok * n_batch, width))
    dwi_ref[0] = dot_tn(all_c, gi_scr[...].reshape(n_tok * n_batch, width))

    for lane in range(0, width, LANES):
        cols = slice(lane, lane + LANES)
        zero8 = jnp.zeros((8, LANES), jnp.float32)
        zero = jnp.zeros((n_batch, LANES), jnp.float32)

        def tap_body(chunk, carry):
            sums = list(carry[:CONV + 1])
            ahead = list(carry[CONV + 1:])
            base = n_tok - STEPS - chunk * STEPS
            for step in reversed(range(STEPS)):
                tok = base + step
                d_conv = d_scr[tok, :, cols]
                sums[CONV] = sums[CONV] + fold_rows(d_conv)
                masked = [d_conv] + [mask_ref[tap - 1, tok] * d_conv for tap in range(1, CONV)]
                for tap in range(CONV):
                    sums[tap] = sums[tap] + fold_rows(masked[tap] * u_scr[tok + HALO - tap, :, cols])
                terms = [par_ref[W0 + tap:W0 + tap + 1, cols] * masked[tap] for tap in range(CONV)]
                a_scr[tok, :, cols] = ahead[0] + terms[0]
                ahead = [ahead[1] + terms[1], ahead[2] + terms[2], terms[3]]
            return tuple(sums) + tuple(ahead)

        out = lax.fori_loop(0, n_tok // STEPS, tap_body, (zero8,) * (CONV + 1) + (zero,) * HALO)
        for row in range(CONV + 1):
            vec_ref[0, GW + row:GW + row + 1, cols] = jnp.sum(out[row], axis=0, keepdims=True)
        for row in range(HALO):
            back_ref[HALO - 1 - row, :, cols] = out[CONV + 1 + row]

    tail_ref[...] = a_scr[n_tok - HALO:]
    for start in range(0, n_tok, 16):
        du_ref[:, start:start + 16, :] = jnp.swapaxes(a_scr[start:start + 16], 0, 1).astype(jnp.bfloat16)


def solution(mesh):
    n_dev = mesh.shape['cp']
    to_next = [(src, src + 1) for src in range(n_dev - 1)]
    to_prev = [(src + 1, src) for src in range(n_dev - 1)]
    seq_spec = P(None, 'cp', None)
    rep_spec = P()

    def local_fn(u_in, seg_ids, grad_h, conv_w, conv_b, a_gate_w, a_gate_b, x_gate_w, x_gate_b, lam_param):
        n_batch, n_tok, n_width = u_in.shape
        n_heads, block_w, _ = a_gate_w.shape
        has_prev = lax.axis_index('cp') > 0
        tail_pack = jnp.concatenate([u_in[:, n_tok - HALO:, :].astype(jnp.float32),
                                     seg_ids[:, n_tok - HALO:, None].astype(jnp.float32)], axis=2)
        recv_pack = lax.ppermute(tail_pack, 'cp', to_next)
        halo_u = jnp.swapaxes(recv_pack[:, :, :n_width], 0, 1)
        halo_seg = recv_pack[:, :, n_width].astype(jnp.int32)
        seg_ext = jnp.concatenate([halo_seg, seg_ids], axis=1).T
        ext_ok = (jnp.arange(n_tok + HALO) >= HALO) | has_prev
        masks = []
        for tap in range(1, CONV):
            tap_ok = (seg_ext[HALO - tap:HALO - tap + n_tok] == seg_ext[HALO:]) & ext_ok[HALO - tap:HALO - tap + n_tok, None]
            masks.append(tap_ok.astype(jnp.float32))
        masks = jnp.broadcast_to(jnp.stack(masks)[..., None], (HALO, n_tok, n_batch, LANES))
        log_rate = -8.0 * jax.nn.softplus(-lam_param)
        par = jnp.concatenate([conv_w, conv_b[None], a_gate_b[None], x_gate_b[None], log_rate[None], log_rate[None] * LOG2E,
                               jnp.zeros((N_PAR - 9, n_width), jnp.float32)], axis=0)

        def blk_row():
            return pl.BlockSpec((n_batch, n_tok, block_w), lambda h: (0, 0, h))

        def blk_time(count):
            return pl.BlockSpec((count, n_batch, block_w), lambda h: (0, 0, h))

        mask_spec = pl.BlockSpec((HALO, n_tok, n_batch, LANES), lambda h: (0, 0, 0, 0))
        mat_spec = pl.BlockSpec((1, block_w, block_w), lambda h: (h, 0, 0))
        par_spec = pl.BlockSpec((N_PAR, block_w), lambda h: (0, h))
        save_spec = pl.BlockSpec((None, n_tok, n_batch, block_w), lambda h: (h, 0, 0, 0))
        save_shape = jax.ShapeDtypeStruct((n_heads, n_tok, n_batch, block_w), jnp.float32)
        f32_scr = pltpu.VMEM((n_tok, n_batch, block_w), jnp.float32)
        bf_scr = pltpu.VMEM((n_tok, n_batch, block_w), jnp.bfloat16)
        u_scr = pltpu.VMEM((n_tok + HALO, n_batch, block_w), jnp.float32)
        limit = pltpu.CompilerParams(vmem_limit_bytes=60 * 2 ** 20)

        sums, sav_c, sav_r, sav_i = pl.pallas_call(
            first_kernel, grid=(n_heads,),
            in_specs=[blk_row(), blk_row(), blk_time(HALO), mask_spec, mat_spec, mat_spec, par_spec],
            out_specs=[blk_time(3), save_spec, save_spec, save_spec],
            out_shape=[jax.ShapeDtypeStruct((3, n_batch, n_width), jnp.float32), save_shape, save_shape, save_shape],
            scratch_shapes=[u_scr, bf_scr, f32_scr, f32_scr, f32_scr, f32_scr],
            compiler_params=limit, name='local_pass',
        )(u_in, grad_h, halo_u, masks, a_gate_w, x_gate_w, par)

        half = n_width * n_batch // n_dev
        mine = lax.all_to_all(sums.reshape(3, n_dev, half), 'cp', split_axis=1, concat_axis=1, tiled=True)
        prods, states, firsts = mine[0], mine[1], mine[2]
        into_state = [jnp.zeros((half,), jnp.float32)]
        for dev in range(n_dev - 1):
            into_state.append(prods[dev] * into_state[-1] + states[dev])
        into_adj = [jnp.zeros((half,), jnp.float32)]
        for dev in range(n_dev - 1, 0, -1):
            into_adj.append(prods[dev] * into_adj[-1] + firsts[dev])
        give = jnp.stack([jnp.stack(into_state), jnp.stack(into_adj[::-1])])
        carry_in = lax.all_to_all(give, 'cp', split_axis=1, concat_axis=1, tiled=True).reshape(2, n_batch, n_width)

        grad_u, tail, back, g_wa, g_wi, vecs = pl.pallas_call(
            second_kernel, grid=(n_heads,),
            in_specs=[blk_row(), blk_row(), blk_time(HALO), mask_spec, mat_spec, mat_spec, par_spec,
                      save_spec, save_spec, save_spec, blk_time(2)],
            out_specs=[blk_row(), blk_time(HALO), blk_time(HALO), mat_spec, mat_spec, pl.BlockSpec((1, N_VEC, block_w), lambda h: (h, 0, 0))],
            out_shape=[jax.ShapeDtypeStruct(u_in.shape, jnp.bfloat16), jax.ShapeDtypeStruct((HALO, n_batch, n_width), jnp.float32),
                       jax.ShapeDtypeStruct((HALO, n_batch, n_width), jnp.float32),
                       jax.ShapeDtypeStruct(a_gate_w.shape, jnp.float32), jax.ShapeDtypeStruct(a_gate_w.shape, jnp.float32),
                       jax.ShapeDtypeStruct((n_heads, N_VEC, block_w), jnp.float32)],
            scratch_shapes=[u_scr, bf_scr, bf_scr, bf_scr] + [f32_scr] * 6,
            compiler_params=limit, name='full_pass',
        )(u_in, grad_h, halo_u, masks, a_gate_w, x_gate_w, par, sav_c, sav_r, sav_i, carry_in)
        halo_back = lax.ppermute(back, 'cp', to_prev)
        return grad_u, tail, halo_back, g_wa, g_wi, vecs

    def full_fn(*args):
        lam_param = args[-1]
        grad_u, tail, halo_back, g_wa, g_wi, vecs = local_fn(*args)
        tail = jnp.swapaxes((tail + halo_back).astype(jnp.bfloat16), 0, 1)
        grad_u = lax.dynamic_update_slice(grad_u, tail, (0, grad_u.shape[1] - HALO, 0))
        g_wa, g_wi, vecs = lax.psum((g_wa, g_wi, vecs), 'cp')
        vecs = jnp.swapaxes(vecs, 0, 1).reshape(N_VEC, -1)
        g_lam = 8.0 * jax.nn.sigmoid(-lam_param) * vecs[GLAM]
        return (grad_u, vecs[GW:GW + CONV], vecs[GBC], g_wa, vecs[GBA], g_wi, vecs[GBI], g_lam)

    return jax.shard_map(full_fn, mesh=mesh,
                         in_specs=(seq_spec, P(None, 'cp'), seq_spec, rep_spec, rep_spec, rep_spec,
                                   rep_spec, rep_spec, rep_spec, rep_spec),
                         out_specs=(seq_spec,) + (rep_spec,) * 7, check_vma=False)
```

time: 2180 us -> 501 us (0.23)
  other arithmetic: 865 us -> 3.27 us
  waiting for transfers between devices: 593 us -> 213 us
  starting transfers between devices: 310 us -> 3.81 us
  local copies, waits for them, and re-layouts: 213 us -> 36 us
  matrix products: 166 us -> 0 us
  Pallas kernels: 0 us -> 154 us
  blocking collectives: 0 us -> 75.2 us
    ppermute x63 -> x1, starting transfers between devices: 306 us -> 1.28 us  [local_fn(): halo_back = lax.ppermute(back, 'cp', to_prev)]
    ppermute x63 -> x1, waiting for transfers between devices: 300 us -> 3.99 us  [local_fn(): halo_back = lax.ppermute(back, 'cp', to_prev)]
    dynamic_update_slice x128 -> x0, other arithmetic: 268 us -> none  [local_fn(): lax.scan(fwd_step, (zero_state, one_state), (decay_a, x_t))]
    mul x68 -> x2, other arithmetic: 216 us -> 0.65 us  [the longest x1 0.63 us: full_fn(): g_lam = 8.0 * jax.nn.sigmoid(-lam_param) * vecs[GLAM]]
    add x64 -> x2, other arithmetic: 171 us -> 0.81 us  [the longest x1 0.42 us: local_fn(): into_adj.append(prods[dev] * into_adj[-1] + firsts[dev])]
    dot_general x6 -> x0, matrix products: 166 us -> none  [the longest x1 59.1 us: local_fn(): jnp.einsum('lbhk,lbhj->hkj', conv_bf, gi_bf, preferred_element_type=jnp.f...]
    pallas_call x0 -> x2, Pallas kernels: none -> 154 us  [the longest x1 87 us: local_fn(): pl.pallas_call(second_kernel, grid=(n_heads,), in_specs=[blk_row(), blk_r...]
    reduce_sum x2 -> x0, other arithmetic: 109 us -> none  [the longest x1 64 us: local_fn(): jnp.sum(d_log * gate_r, axis=(0, 1))]
  transfers between devices with their start and end apart: 66 -> 3, of which waited for: 64 -> 3; matrix products, arithmetic and copies ran while one was open for 6% -> 2% of each run, Pallas kernels for 0% -> 0%
where the time goes in v1:
time: 501 us; the launch traced here: 500 us
  waiting for transfers between devices  213 us (43%)
  Pallas kernels  154 us (31%)
  blocking collectives  75.2 us (15%)
  local copies, waits for them, and re-layouts  36 us (7%)
  between operations  14.3 us (3%)
    psum x1, waiting for transfers between devices, full_fn(): g_wa, g_wi, vecs = lax.psum((g_wa, g_wi, vecs), 'cp')  209 us
    pallas_call x1, Pallas kernels, local_fn(): pl.pallas_call(second_kernel, grid=(n_heads,), in_specs=[blk_row(), blk_r...  87 us
    pallas_call x1, Pallas kernels, local_fn(): pl.pallas_call(first_kernel, grid=(n_heads,), in_specs=[blk_row(), blk_ro...  67.3 us
    all_to_all x1, blocking collectives, local_fn(): lax.all_to_all(sums.reshape(3, n_dev, half), 'cp', split_axis=1, concat_a...  52.3 us
    all_to_all x1, blocking collectives, local_fn(): lax.all_to_all(give, 'cp', split_axis=1, concat_axis=1, tiled=True)  22.9 us
  transfers between devices with their start and end apart: 3, of which 3 were waited for; matrix products, arithmetic and copies ran while one was open for 2% of the time, Pallas kernels for 0%

profile of v1, /device:TPU:0, one launch (start us, length us, event | category | flops | bytes accessed | tf_op | source)
XLA Modules:
  0.0 500.0 jit_solution(879352502679695341)
XLA Ops:
  7.3 0.8 slice_convert_fusion.1
  8.2 1.7 slice.560
  10.1 2.5 collective-permute-start
  12.8 1.5 concatenate.11.par_ref
  15.3 1.0 slice_bitcast_fusion.halo_ref
  16.3 1.6 broadcast_in_dim.12.mask_ref
  18.0 67.3 %local_pass.1 = (f32[3,16,5376]{2,1,0:T(8,128)}, f32[21,64,16,256]{3,2,1,0:T(8,128)}, f32[21,64,16,256]{3,2,1,0:T(8,128)}, f32[21,64,16,256]{3,2,1,0:T(8,128)}) custom-call(bf16[16,64,5376]{2,1,0:T(8,128)(2,1)} %u_ref.3, f32[16,64,5376]{2,1,0:T(8,128)} %gh_ref.3, f32[3,16,5376]{2,1,0:T(8,128)} %slice_bitcast_fusion.halo_ref, ...), custom_call_target="tpu_custom_call" | custom-call | tf_op jit(solution)/shard_map/local_pass/pallas_call | solution.py:261
  85.3 1.4 reshape.8913
  86.7 0.7 copy.44
  87.4 52.3 %all_to_all.10 = f32[3,32,2688]{2,0,1:T(4,128)S(1)} all-to-all(f32[3,32,2688]{2,0,1:T(4,128)S(1)} %copy.44), channel_id=1, replica_groups=mesh['cp'=32] {'cp'}, dimensions={1} | all-to-all | bytes 2064384 | tf_op jit(solution)/shard_map/all_to_all | solution.py:271
  139.7 0.4 fusion.32
  140.1 0.5 stack.29
  141.0 0.4 fusion.1
  141.4 0.5 stack.31
  142.2 0.6 pad_maximum_fusion.1
  142.9 22.9 %all_to_all.11 = f32[2,32,2688]{2,0,1:T(2,128)S(1)} all-to-all(f32[2,32,2688]{2,0,1:T(2,128)S(1)} %pad_maximum_fusion.1), channel_id=1, replica_groups=mesh['cp'=32] {'cp'}, dimensions={1} | all-to-all | bytes 1376256 | tf_op jit(solution)/shard_map/all_to_all | solution.py:280
  165.9 1.0 reshape.8914.in_ref
  166.9 87.0 %full_pass.1 = (bf16[16,64,5376]{2,1,0:T(8,128)(2,1)}, f32[3,16,5376]{2,1,0:T(8,128)}, f32[3,16,5376]{2,1,0:T(8,128)}, f32[21,256,256]{2,1,0:T(8,128)}, f32[21,256,256]{2,1,0:T(8,128)}, /*index=5*/f32[21,8,256]{2,1,0:T(8,128)}) custom-call(bf16[16,64,5376]{2,1,0:T(8,128)(2,1)} %u_ref.3, f32[16,64,5376]{2,1,0:T(8,128)} %gh_ref.3, ...), custom_call_target="tpu_custom_call" | custom-call | tf_op jit(solution)/shard_map/full_pass/pallas_call | solution.py:282
  253.9 1.2 copy-done.7
  255.1 1.3 collective-permute-start.1
  256.4 4.0 collective-permute-done.1
  260.5 0.4 copy.47
  260.8 9.8 %dynamic_update_slice.3 = bf16[16,64,5376]{2,1,0:T(8,128)(2,1)} dynamic-update-slice(bf16[16,64,5376]{2,1,0:T(8,128)(2,1)} %get-tuple-element.22, bf16[16,3,5376]{2,1,0:T(4,128)(2,1)S(1)} %copy.47, s32[]{:T(128)} %constant.11.clone.1, s32[]{:T(128)} %constant.5.clone.1, s32[]{:T(128)} %constant.11.clone.1) | dynamic-update-slice | bytes 1032196 | tf_op jit(solution)/shard_map/dynamic_update_slice | solution.py:301
  270.6 208.7 %all-reduce.3.cloned.1.call-done = (f32[8,21,256]{2,0,1:T(8,128)}, f32[21,256,256]{2,1,0:T(8,128)}, f32[21,256,256]{2,1,0:T(8,128)}) async-done(((f32[8,21,256]{2,0,1:T(8,128)}, f32[21,256,256]{2,1,0:T(8,128)}, f32[21,256,256]{2,1,0:T(8,128)}), (f32[8,21,256]{2,0,1:T(8,128)}, f32[21,256,256]{2,1,0:T(8,128)}, f32[21,256,256]{2,1,0:T(8,128)})) %all-reduce.3.cloned.1.call-update) | async-done | bytes 11182096 | tf_op jit(solution)/shard_map/psum | solution.py:302
  479.3 1.6 slice.771
  480.9 1.6 slice_reduce_fusion
  482.5 0.6 multiply_multiply_fusion
  483.2 0.6 squeeze.412
  483.8 0.6 squeeze.411
  484.4 0.6 squeeze.410
  485.0 5.7 %copy.57 = f32[21,256,256]{2,1,0:T(8,128)} copy(f32[21,256,256]{2,1,0:T(8,128)} %get-tuple-element.108) | data formatting | bytes 11010048
  490.7 2.4 copy.58
  (48 shorter events, 2.2 us)
Async XLA Ops:
  7.2 5.4 %copy-start.4 = (f32[5376]{0:T(1024)S(1)}, f32[5376]{0:T(1024)}, u32[]{:S(2)}) copy-start(f32[5376]{0:T(1024)} %param.14) | copy-start | bytes 64516
  7.2 5.5 %copy-start.5 = (f32[5376]{0:T(1024)S(1)}, f32[5376]{0:T(1024)}, u32[]{:S(2)}) copy-start(f32[5376]{0:T(1024)} %param.16) | copy-start | bytes 64516
  7.2 5.5 %copy-start.6 = (f32[5376]{0:T(1024)S(1)}, f32[5376]{0:T(1024)}, u32[]{:S(2)}) copy-start(f32[5376]{0:T(1024)} %param.18) | copy-start | bytes 64516
  7.2 5.5 %copy-start.1 = (f32[5376]{0:T(1024)S(1)}, f32[5376]{0:T(1024)}, u32[]{:S(2)}) copy-start(f32[5376]{0:T(1024)} %param.19) | copy-start | bytes 64516
  7.2 472.1 %all-reduce.3.cloned.1.call-start = ((), (), s32[]{:S(2)}) async-start(), calls=%async_computation.2 | async-start | bytes 22364160 | tf_op jit(solution)/shard_map/psum | solution.py:302
  8.2 4.6 copy-start.2
  9.9 5.1 %copy-start.3 = (s32[16,64]{1,0:T(8,128)S(1)}, s32[16,64]{1,0:T(8,128)}, u32[]{:S(2)}) copy-start(s32[16,64]{1,0:T(8,128)} %param.11) | copy-start | bytes 12292
  10.1 4.7 collective-permute-start
  253.9 1.2 copy-start.7
  253.9 6.5 %copy-start = (f32[3,16,5376]{2,1,0:T(8,128)S(1)}, f32[3,16,5376]{2,1,0:T(8,128)}, u32[]{:S(2)}) copy-start(f32[3,16,5376]{2,1,0:T(8,128)} %get-tuple-element.23) | copy-start | bytes 3096580
  255.1 5.3 %collective-permute-start.1 = (f32[3,16,5376]{2,1,0:T(8,128)S(1)}, f32[3,16,5376]{2,1,0:T(8,128)S(1)}, u32[]{:S(2)}, u32[]{:S(2)}) collective-permute-start(f32[3,16,5376]{2,1,0:T(8,128)S(1)} %copy-done.7), channel_id=1, source_target_pairs={{1,0},{2,1},{3,2},{4,3},{5,4},{6,5},{7,6},{8,7},{9,8},{10,9},{11,1... | collective-permute-start | bytes 3096584 | tf_op jit(solution)/shard_map/ppermute | solution.py:294
  483.2 7.5 %slice-start = ((s8[5505024]{0:T(1024)(128)(4,1)}), s8[1310720]{0:T(1024)(128)(4,1)S(1)}, s32[]{:S(2)}) async-start(s8[5505024]{0:T(1024)(128)(4,1)} %bitcast.559), calls=%async_computation.3 | async-start | bytes 2621440
  485.0 5.7 %slice-start.1 = ((s8[5505024]{0:T(1024)(128)(4,1)}), s8[4194304]{0:T(1024)(128)(4,1)S(1)}, s32[]{:S(2)}) async-start(s8[5505024]{0:T(1024)(128)(4,1)} %bitcast.559), calls=%async_computation.4 | async-start | bytes 8388608
Sparse Core Ops, SparseCore 0:
  254.0 225.2 all-reduce.2

commit v2 on v0

v2 whole, which is shorter than its diff:
```python
import functools

import jax
import jax.numpy as jnp
from jax import lax
from jax.experimental import pallas as pl
from jax.experimental.pallas import tpu as pltpu
from jax.sharding import PartitionSpec as P

CONV = 4
HALO = CONV - 1
LOG2E = 1.4426950408889634
LANES = 128
STEPS = 8
LAG = 2
SLOTS = LAG + 1
ROWS = 8

W0, BC, BA, BI, KL, KE = 0, 4, 5, 6, 7, 8
N_PAR = 16
GW, GBC, GBA, GBI, GLAM = 0, 4, 5, 6, 7
N_VEC = 8


def sigmoid_of(pre):
    root = lax.rsqrt(1.0 + jnp.exp2(pre * (-LOG2E)))
    return root * root


def decay_of(gate_r, par_kl, par_ke, keep):
    a_raw = jnp.exp2(gate_r * par_ke)
    gap = jnp.tanh(gate_r * (-par_kl)) * (1.0 + a_raw * a_raw)
    inv_root = lax.rsqrt(gap)
    decay = a_raw * keep
    mult = jnp.where(keep > 0.5, gap * inv_root, 1.0)
    return decay, mult, decay * decay * inv_root


def fold_rows(arr):
    return arr[:8] + arr[8:]


def dot_nn(lhs, rhs):
    return lax.dot_general(lhs, rhs, (((1,), (0,)), ((), ())), preferred_element_type=jnp.float32)


def dot_nt(lhs, rhs):
    return lax.dot_general(lhs, rhs, (((1,), (1,)), ((), ())), preferred_element_type=jnp.float32)


def dot_tn(lhs, rhs):
    return lax.dot_general(lhs, rhs, (((0,), (0,)), ((), ())), preferred_element_type=jnp.float32)


def fused_kernel(n_dev, n_heads,
                 u_ref, gh_ref, halo_ref, mask_ref, wa_ref, wi_ref, wa2_ref, wi2_ref, par_ref, par2_ref,
                 du_ref, tail_ref, back_ref, dwa_ref, dwi_ref, vec_ref,
                 u_s, c_s, r_s, i_s, a_s, m_s, e_s, g_s, cb_s, h_scr, d_scr, ga_scr, gi_scr,
                 send, recv, resp, carry, send_sem, recv_sem, give_sem, take_sem):
    n_batch, n_tok, width = u_ref.shape
    step_id = pl.program_id(0)
    me = lax.axis_index('cp')
    rows = 256
    span = rows // n_batch

    def spread(src, dst, out_sem, in_sem, head, count):
        def one(k, _):
            dev = lax.rem(me + k, n_dev)
            pltpu.make_async_remote_copy(
                src_ref=src.at[head, pl.ds(pl.multiple_of(dev * ROWS, ROWS), count)],
                dst_ref=dst.at[head, pl.ds(pl.multiple_of(me * ROWS, ROWS), count)],
                send_sem=out_sem.at[head], recv_sem=in_sem.at[head],
                device_id=(dev,), device_id_type=pl.DeviceIdType.MESH).start()
            return 0
        lax.fori_loop(1, n_dev, one, 0)
        own = pl.ds(pl.multiple_of(me * ROWS, ROWS), ROWS)
        dst[head, own, :] = src[head, own, :]

    def settle(buf, sem, head, count):
        total = buf.at[head, pl.ds(0, (n_dev - 1) * count)]
        pltpu.make_async_copy(total, total, sem.at[head]).wait()

    @pl.when((step_id >= 1) & (step_id <= n_heads))
    def _combine():
        head = step_id - 1
        settle(recv, recv_sem, head, 3)
        state = jnp.zeros((1, LANES), jnp.float32)
        adj = jnp.zeros((1, LANES), jnp.float32)
        for dev in range(n_dev):
            row, back_row = dev * ROWS, (n_dev - 1 - dev) * ROWS
            resp[head, row:row + 1, :] = state
            resp[head, back_row + 1:back_row + 2, :] = adj
            state = recv[head, row:row + 1, :] * state + recv[head, row + 1:row + 2, :]
            adj = recv[head, back_row:back_row + 1, :] * adj + recv[head, back_row + 2:back_row + 3, :]
        spread(resp, carry, give_sem, take_sem, head, 2)

    @pl.when(step_id < n_heads)
    def _first():
        head = step_id
        slot = lax.rem(step_id, SLOTS)
        u_s[slot, :HALO] = halo_ref[...]
        for start in range(0, n_tok, 16):
            u_s[slot, HALO + start:HALO + start + 16] = jnp.swapaxes(u_ref[:, start:start + 16, :].astype(jnp.float32), 0, 1)
        for start in range(0, n_tok, 8):
            g_s[slot, start:start + 8] = jnp.swapaxes(gh_ref[:, start:start + 8, :], 0, 1)

        def conv_body(chunk, _):
            base = chunk * STEPS
            for step in range(STEPS):
                tok = base + step
                for lane in range(0, width, LANES):
                    cols = slice(lane, lane + LANES)
                    acc = par_ref[BC:BC + 1, cols] + par_ref[W0:W0 + 1, cols] * u_s[slot, tok + HALO, :, cols]
                    for tap in range(1, CONV):
                        acc = acc + par_ref[W0 + tap:W0 + tap + 1, cols] * (mask_ref[tap - 1, tok] * u_s[slot, tok + HALO - tap, :, cols])
                    c_s[slot, tok, :, cols] = acc
                    cb_s[slot, tok, :, cols] = acc.astype(jnp.bfloat16)
            return 0

        lax.fori_loop(0, n_tok // STEPS, conv_body, 0)
        for start in range(0, n_tok, span):
            part = cb_s[slot, start:start + span].reshape(rows, width)
            r_s[slot, start:start + span] = dot_nn(part, wa_ref[0]).reshape(span, n_batch, width)
            i_s[slot, start:start + span] = dot_nn(part, wi_ref[0]).reshape(span, n_batch, width)

        for half in range(width // LANES):
            cols = slice(half * LANES, (half + 1) * LANES)

            def fwd_body(chunk, run):
                state, prod = run
                base = chunk * STEPS
                for step in range(STEPS):
                    tok = base + step
                    gate_r = sigmoid_of(r_s[slot, tok, :, cols] + par_ref[BA:BA + 1, cols])
                    gate_i = sigmoid_of(i_s[slot, tok, :, cols] + par_ref[BI:BI + 1, cols])
                    decay, mult, ratio = decay_of(gate_r, par_ref[KL:KL + 1, cols], par_ref[KE:KE + 1, cols], mask_ref[0, tok])
                    r_s[slot, tok, :, cols] = gate_r
                    i_s[slot, tok, :, cols] = gate_i
                    a_s[slot, tok, :, cols] = decay
                    m_s[slot, tok, :, cols] = mult
                    e_s[slot, tok, :, cols] = ratio
                    state = decay * state + mult * (gate_i * c_s[slot, tok, :, cols])
                    prod = decay * prod
                return state, prod

            zero = jnp.zeros((n_batch, LANES), jnp.float32)
            state, prod = lax.fori_loop(0, n_tok // STEPS, fwd_body, (zero, zero + 1.0))

            def adj_body(chunk, adj):
                base = n_tok - STEPS - chunk * STEPS
                for step in reversed(range(STEPS)):
                    tok = base + step
                    adj = a_s[slot, tok, :, cols] * (g_s[slot, tok, :, cols] + adj)
                return adj

            first = lax.fori_loop(0, n_tok // STEPS, adj_body, zero)
            for row, val in enumerate((prod, state, first)):
                send.at[head][pl.ds(half * ROWS + row, n_batch, stride=2 * ROWS), :] = val
        spread(send, recv, send_sem, recv_sem, head, 3)

    @pl.when(step_id >= LAG)
    def _second():
        head = step_id - LAG
        slot = lax.rem(step_id - LAG, SLOTS)
        settle(carry, take_sem, head, 2)

        for half in range(width // LANES):
            cols = slice(half * LANES, (half + 1) * LANES)
            zero8 = jnp.zeros((8, LANES), jnp.float32)

            def fwd_body(chunk, state):
                base = chunk * STEPS
                for step in range(STEPS):
                    tok = base + step
                    h_scr[tok, :, cols] = state
                    state = a_s[slot, tok, :, cols] * state + m_s[slot, tok, :, cols] * (i_s[slot, tok, :, cols] * c_s[slot, tok, :, cols])
                return state

            lax.fori_loop(0, n_tok // STEPS, fwd_body, carry.at[head][pl.ds(half * ROWS, n_batch, stride=2 * ROWS), :])

            def bwd_body(chunk, run):
                adj_next, sum_a, sum_i, sum_l = run
                base = n_tok - STEPS - chunk * STEPS
                for step in reversed(range(STEPS)):
                    tok = base + step
                    gate_r = r_s[slot, tok, :, cols]
                    gate_i = i_s[slot, tok, :, cols]
                    conv_c = c_s[slot, tok, :, cols]
                    adj = g_s[slot, tok, :, cols] + adj_next
                    adj_next = a_s[slot, tok, :, cols] * adj
                    d_log = adj_next * h_scr[tok, :, cols] - adj * (gate_i * conv_c) * e_s[slot, tok, :, cols]
                    direct = adj * m_s[slot, tok, :, cols] * gate_i
                    d_pre_i = direct * conv_c * (1.0 - gate_i)
                    d_log_r = d_log * gate_r
                    d_pre_a = d_log_r * (par2_ref[KL:KL + 1, cols] * (1.0 - gate_r))
                    sum_l = sum_l + fold_rows(d_log_r)
                    sum_a = sum_a + fold_rows(d_pre_a)
                    sum_i = sum_i + fold_rows(d_pre_i)
                    d_scr[tok, :, cols] = direct
                    ga_scr[tok, :, cols] = d_pre_a.astype(jnp.bfloat16)
                    gi_scr[tok, :, cols] = d_pre_i.astype(jnp.bfloat16)
                return adj_next, sum_a, sum_i, sum_l

            adj_in = carry.at[head][pl.ds(half * ROWS + 1, n_batch, stride=2 * ROWS), :]
            _, sum_a, sum_i, sum_l = lax.fori_loop(0, n_tok // STEPS, bwd_body, (adj_in, zero8, zero8, zero8))
            vec_ref[0, GBA:GBA + 1, cols] = jnp.sum(sum_a, axis=0, keepdims=True)
            vec_ref[0, GBI:GBI + 1, cols] = jnp.sum(sum_i, axis=0, keepdims=True)
            vec_ref[0, GLAM:GLAM + 1, cols] = jnp.sum(sum_l, axis=0, keepdims=True)

        for start in range(0, n_tok, span):
            toks = slice(start, start + span)
            back = dot_nt(ga_scr[toks].reshape(rows, width), wa2_ref[0]) + dot_nt(gi_scr[toks].reshape(rows, width), wi2_ref[0])
            d_scr[toks] = d_scr[toks] + back.reshape(span, n_batch, width)
        all_c = cb_s[slot].reshape(n_tok * n_batch, width)
        dwa_ref[0] = dot_tn(all_c, ga_scr[...].reshape(n_tok * n_batch, width))
        dwi_ref[0] = dot_tn(all_c, gi_scr[...].reshape(n_tok * n_batch, width))

        for half in range(width // LANES):
            cols = slice(half * LANES, (half + 1) * LANES)
            zero8 = jnp.zeros((8, LANES), jnp.float32)
            zero = jnp.zeros((n_batch, LANES), jnp.float32)

            def tap_body(chunk, run):
                sums = list(run[:CONV + 1])
                ahead = list(run[CONV + 1:])
                base = n_tok - STEPS - chunk * STEPS
                for step in reversed(range(STEPS)):
                    tok = base + step
                    d_conv = d_scr[tok, :, cols]
                    sums[CONV] = sums[CONV] + fold_rows(d_conv)
                    masked = [d_conv] + [mask_ref[tap - 1, tok] * d_conv for tap in range(1, CONV)]
                    for tap in range(CONV):
                        sums[tap] = sums[tap] + fold_rows(masked[tap] * u_s[slot, tok + HALO - tap, :, cols])
                    terms = [par2_ref[W0 + tap:W0 + tap + 1, cols] * masked[tap] for tap in range(CONV)]
                    h_scr[tok, :, cols] = ahead[0] + terms[0]
                    ahead = [ahead[1] + terms[1], ahead[2] + terms[2], terms[3]]
                return tuple(sums) + tuple(ahead)

            out = lax.fori_loop(0, n_tok // STEPS, tap_body, (zero8,) * (CONV + 1) + (zero,) * HALO)
            for row in range(CONV + 1):
                vec_ref[0, GW + row:GW + row + 1, cols] = jnp.sum(out[row], axis=0, keepdims=True)
            for row in range(HALO):
                back_ref[HALO - 1 - row, :, cols] = out[CONV + 1 + row]

        tail_ref[...] = h_scr[n_tok - HALO:]
        for start in range(0, n_tok, 16):
            du_ref[:, start:start + 16, :] = jnp.swapaxes(h_scr[start:start + 16], 0, 1).astype(jnp.bfloat16)

    @pl.when(step_id == n_heads - 1 + LAG)
    def _drain():
        def one(head, _):
            settle(send, send_sem, head, 3)
            settle(resp, give_sem, head, 2)
            return 0
        lax.fori_loop(0, n_heads, one, 0)


def solution(mesh):
    n_dev = mesh.shape['cp']
    to_next = [(src, src + 1) for src in range(n_dev - 1)]
    to_prev = [(src + 1, src) for src in range(n_dev - 1)]
    seq_spec = P(None, 'cp', None)
    rep_spec = P()

    def local_fn(u_in, seg_ids, grad_h, conv_w, conv_b, a_gate_w, a_gate_b, x_gate_w, x_gate_b, lam_param):
        n_batch, n_tok, n_width = u_in.shape
        n_heads, block_w, _ = a_gate_w.shape
        has_prev = lax.axis_index('cp') > 0
        tail_pack = jnp.concatenate([u_in[:, n_tok - HALO:, :].astype(jnp.float32),
                                     seg_ids[:, n_tok - HALO:, None].astype(jnp.float32)], axis=2)
        recv_pack = lax.ppermute(tail_pack, 'cp', to_next)
        halo_u = jnp.swapaxes(recv_pack[:, :, :n_width], 0, 1)
        halo_seg = recv_pack[:, :, n_width].astype(jnp.int32)
        seg_ext = jnp.concatenate([halo_seg, seg_ids], axis=1).T
        ext_ok = (jnp.arange(n_tok + HALO) >= HALO) | has_prev
        masks = []
        for tap in range(1, CONV):
            tap_ok = (seg_ext[HALO - tap:HALO - tap + n_tok] == seg_ext[HALO:]) & ext_ok[HALO - tap:HALO - tap + n_tok, None]
            masks.append(tap_ok.astype(jnp.float32))
        masks = jnp.broadcast_to(jnp.stack(masks)[..., None], (HALO, n_tok, n_batch, LANES))
        log_rate = -8.0 * jax.nn.softplus(-lam_param)
        par = jnp.concatenate([conv_w, conv_b[None], a_gate_b[None], x_gate_b[None], log_rate[None], log_rate[None] * LOG2E,
                               jnp.zeros((N_PAR - 9, n_width), jnp.float32)], axis=0)

        def now(step):
            return jnp.minimum(step, n_heads - 1)

        def late(step):
            return jnp.maximum(step - LAG, 0)

        def blk_row(at):
            return pl.BlockSpec((n_batch, n_tok, block_w), lambda s: (0, 0, at(s)))

        def blk_time(count, at):
            return pl.BlockSpec((count, n_batch, block_w), lambda s: (0, 0, at(s)))

        def mat_spec(at):
            return pl.BlockSpec((1, block_w, block_w), lambda s: (at(s), 0, 0))

        def par_spec(at):
            return pl.BlockSpec((N_PAR, block_w), lambda s: (0, at(s)))

        mask_spec = pl.BlockSpec((HALO, n_tok, n_batch, LANES), lambda s: (0, 0, 0, 0))
        f32_slots = pltpu.VMEM((SLOTS, n_tok, n_batch, block_w), jnp.float32)
        f32_scr = pltpu.VMEM((n_tok, n_batch, block_w), jnp.float32)
        bf_scr = pltpu.VMEM((n_tok, n_batch, block_w), jnp.bfloat16)
        wire = pltpu.VMEM((n_heads, n_dev * ROWS, LANES), jnp.float32)
        sems = pltpu.SemaphoreType.DMA((n_heads,))

        grad_u, tail, back, g_wa, g_wi, vecs = pl.pallas_call(
            functools.partial(fused_kernel, n_dev, n_heads), grid=(n_heads + LAG,),
            in_specs=[blk_row(now), blk_row(now), blk_time(HALO, now), mask_spec, mat_spec(now), mat_spec(now),
                      mat_spec(late), mat_spec(late), par_spec(now), par_spec(late)],
            out_specs=[blk_row(late), blk_time(HALO, late), blk_time(HALO, late), mat_spec(late), mat_spec(late),
                       pl.BlockSpec((1, N_VEC, block_w), lambda s: (late(s), 0, 0))],
            out_shape=[jax.ShapeDtypeStruct(u_in.shape, jnp.bfloat16), jax.ShapeDtypeStruct((HALO, n_batch, n_width), jnp.float32),
                       jax.ShapeDtypeStruct((HALO, n_batch, n_width), jnp.float32),
                       jax.ShapeDtypeStruct(a_gate_w.shape, jnp.float32), jax.ShapeDtypeStruct(a_gate_w.shape, jnp.float32),
                       jax.ShapeDtypeStruct((n_heads, N_VEC, block_w), jnp.float32)],
            scratch_shapes=[pltpu.VMEM((SLOTS, n_tok + HALO, n_batch, block_w), jnp.float32)] + [f32_slots] * 7
            + [pltpu.VMEM((SLOTS, n_tok, n_batch, block_w), jnp.bfloat16), f32_scr, f32_scr, bf_scr, bf_scr]
            + [wire] * 4 + [sems] * 4,
            compiler_params=pltpu.CompilerParams(vmem_limit_bytes=63 * 2 ** 20, has_side_effects=True), name='fused_pass',
        )(u_in, grad_h, halo_u, masks, a_gate_w, x_gate_w, a_gate_w, x_gate_w, par, par)
        halo_back = lax.ppermute(back, 'cp', to_prev)
        return grad_u, tail, halo_back, g_wa, g_wi, vecs

    def full_fn(*args):
        lam_param = args[-1]
        grad_u, tail, halo_back, g_wa, g_wi, vecs = local_fn(*args)
        tail = jnp.swapaxes((tail + halo_back).astype(jnp.bfloat16), 0, 1)
        grad_u = lax.dynamic_update_slice(grad_u, tail, (0, grad_u.shape[1] - HALO, 0))
        g_wa, g_wi, vecs = lax.psum((g_wa, g_wi, vecs), 'cp')
        vecs = jnp.swapaxes(vecs, 0, 1).reshape(N_VEC, -1)
        g_lam = 8.0 * jax.nn.sigmoid(-lam_param) * vecs[GLAM]
        return (grad_u, vecs[GW:GW + CONV], vecs[GBC], g_wa, vecs[GBA], g_wi, vecs[GBI], g_lam)

    return jax.shard_map(full_fn, mesh=mesh,
                         in_specs=(seq_spec, P(None, 'cp'), seq_spec, rep_spec, rep_spec, rep_spec,
                                   rep_spec, rep_spec, rep_spec, rep_spec),
                         out_specs=(seq_spec,) + (rep_spec,) * 7, check_vma=False)
```

time: 2180 us -> 479 us (0.22)
  other arithmetic: 865 us -> 2.63 us
  waiting for transfers between devices: 593 us -> 214 us
  starting transfers between devices: 310 us -> 3.81 us
  Pallas kernels: 0 us -> 201 us
  local copies, waits for them, and re-layouts: 213 us -> 42.7 us
  matrix products: 166 us -> 0 us
    ppermute x63 -> x1, starting transfers between devices: 306 us -> 1.28 us  [local_fn(): halo_back = lax.ppermute(back, 'cp', to_prev)]
    ppermute x63 -> x1, waiting for transfers between devices: 300 us -> 3.37 us  [local_fn(): halo_back = lax.ppermute(back, 'cp', to_prev)]
    dynamic_update_slice x128 -> x0, other arithmetic: 268 us -> none  [local_fn(): lax.scan(fwd_step, (zero_state, one_state), (decay_a, x_t))]
    mul x68 -> x2, other arithmetic: 216 us -> 1.39 us  [the longest x1 0.76 us: local_fn(): log_rate[None] * LOG2E]
    pallas_call x0 -> x1, Pallas kernels: none -> 201 us  [local_fn(): pl.pallas_call(functools.partial(fused_kernel, n_dev, n_heads), grid=(n_h...]
    add x64 -> x0, other arithmetic: 171 us -> none  [the longest x31 57.7 us: fwd_chain(): return lax.ppermute(end_prod * state_cur + end_state, 'cp', to_next)]
    dot_general x6 -> x0, matrix products: 166 us -> none  [the longest x1 59.1 us: local_fn(): jnp.einsum('lbhk,lbhj->hkj', conv_bf, gi_bf, preferred_element_type=jnp.f...]
    reduce_sum x2 -> x0, other arithmetic: 109 us -> none  [the longest x1 64 us: local_fn(): jnp.sum(d_log * gate_r, axis=(0, 1))]
  transfers between devices with their start and end apart: 66 -> 3, of which waited for: 64 -> 2; matrix products, arithmetic and copies ran while one was open for 6% -> 3% of each run, Pallas kernels for 0% -> 0%
where the time goes in v2:
time: 479 us; the launch traced here: 478 us
  waiting for transfers between devices  214 us (45%)
  Pallas kernels  201 us (42%)
  local copies, waits for them, and re-layouts  42.7 us (9%)
  between operations  14.2 us (3%)
    psum x1, waiting for transfers between devices, full_fn(): g_wa, g_wi, vecs = lax.psum((g_wa, g_wi, vecs), 'cp')  211 us
    pallas_call x1, Pallas kernels, local_fn(): pl.pallas_call(functools.partial(fused_kernel, n_dev, n_heads), grid=(n_h...  201 us
    unnamed x18, local copies, waits for them, and re-layouts  19.1 us
    dynamic_update_slice x1, local copies, waits for them, and re-layouts, full_fn(): lax.dynamic_update_slice(grad_u, tail, (0, grad_u.shape[1] - HALO, 0))  9.66 us
  transfers between devices with their start and end apart: 3, of which 2 were waited for; matrix products, arithmetic and copies ran while one was open for 3% of the time, Pallas kernels for 0%

profile of v2, /device:TPU:0, one launch (start us, length us, event | category | flops | bytes accessed | tf_op | source)
XLA Modules:
  0.0 478.3 jit_solution(16623354581988383689)
XLA Ops:
  7.2 0.8 slice_convert_fusion.1
  8.0 0.1 copy.39
  8.1 0.1 copy.32
  8.2 1.7 slice.57
  10.1 2.5 collective-permute-start
  12.6 0.8 broadcast_in_dim.13
  13.3 0.8 broadcast_in_dim.28
  14.1 0.8 broadcast_in_dim.29
  14.8 0.8 broadcast_multiply_fusion
  15.7 1.5 concatenate.11.par_ref.par2_ref
  17.2 0.1 fusion.7
  17.3 0.2 copy.36
  17.7 0.1 copy.34
  17.8 1.0 slice_bitcast_fusion.halo_ref
  18.8 1.6 broadcast_in_dim.12.mask_ref
  20.4 200.8 %fused_pass.1 = (bf16[16,64,5376]{2,1,0:T(8,128)(2,1)}, f32[3,16,5376]{2,1,0:T(8,128)}, f32[3,16,5376]{2,1,0:T(8,128)}, f32[21,256,256]{2,1,0:T(8,128)}, f32[21,256,256]{2,1,0:T(8,128)}, /*index=5*/f32[21,8,256]{2,1,0:T(8,128)}) custom-call(bf16[16,64,5376]{2,1,0:T(8,128)(2,1)} %u_ref.1, f32[16,64,5376]{2,1,0:T(8,128)} %gh_ref.1, ...), custom_call_target="tpu_custom_call" | custom-call | tf_op jit(solution)/shard_map/fused_pass/pallas_call | solution.py:310
  221.3 1.2 copy-done.4
  222.4 1.3 collective-permute-start.1
  223.7 3.4 collective-permute-done.1
  227.1 0.1 fusion
  227.2 0.4 copy.35
  227.6 9.7 %dynamic_update_slice.3 = bf16[16,64,5376]{2,1,0:T(8,128)(2,1)} dynamic-update-slice(bf16[16,64,5376]{2,1,0:T(8,128)(2,1)} %get-tuple-element.14, bf16[16,3,5376]{2,1,0:T(4,128)(2,1)S(1)} %copy.35, s32[]{:T(128)} %constant.3.clone.1, s32[]{:T(128)} %constant.7.clone.1, s32[]{:T(128)} %constant.3.clone.1) | dynamic-update-slice | bytes 1032196 | tf_op jit(solution)/shard_map/dynamic_update_slice | solution.py:332
  237.3 210.7 %all-reduce.3.cloned.1.call-done = (f32[8,21,256]{2,0,1:T(8,128)}, f32[21,256,256]{2,1,0:T(8,128)}, f32[21,256,256]{2,1,0:T(8,128)}) async-done(((f32[8,21,256]{2,0,1:T(8,128)}, f32[21,256,256]{2,1,0:T(8,128)}, f32[21,256,256]{2,1,0:T(8,128)}), (f32[8,21,256]{2,0,1:T(8,128)}, f32[21,256,256]{2,1,0:T(8,128)}, f32[21,256,256]{2,1,0:T(8,128)})) %all-reduce.3.cloned.1.call-update) | async-done | bytes 11182096 | tf_op jit(solution)/shard_map/psum | solution.py:333
  448.0 1.6 slice.80
  449.6 1.5 slice_reduce_fusion
  451.1 0.6 squeeze.13
  451.7 0.6 squeeze.14
  452.3 0.6 squeeze.15
  452.9 0.6 multiply_multiply_fusion
  453.6 9.9 %copy.48 = bf16[16,64,5376]{2,1,0:T(8,128)(2,1)} copy(bf16[16,64,5376]{2,1,0:T(8,128)(2,1)} %dynamic_update_slice.3) | data formatting | bytes 22020096
  463.4 5.6 %copy.49 = f32[21,256,256]{2,1,0:T(8,128)} copy(f32[21,256,256]{2,1,0:T(8,128)} %get-tuple-element.46) | data formatting | bytes 11010048
  469.0 2.4 copy.50
  (28 shorter events, 0.5 us)
Async XLA Ops:
  7.2 10.4 %copy-start.3 = (s32[16,64]{1,0:T(8,128)S(1)}, s32[16,64]{1,0:T(8,128)}, u32[]{:S(2)}) copy-start(s32[16,64]{1,0:T(8,128)} %param.11) | copy-start | bytes 12292
  7.2 8.5 %copy-start.2 = (f32[4,5376]{1,0:T(4,128)S(1)}, f32[4,5376]{1,0:T(4,128)}, u32[]{:S(2)}) copy-start(f32[4,5376]{1,0:T(4,128)} %param.13) | copy-start | bytes 258052
  7.2 440.8 %all-reduce.3.cloned.1.call-start = ((), (), s32[]{:S(2)}) async-start(), calls=%async_computation | async-start | bytes 22364160 | tf_op jit(solution)/shard_map/psum | solution.py:333
  10.1 7.3 %collective-permute-start = (f32[16,3,5377]{2,0,1:T(8,128)S(1)}, f32[16,3,5377]{2,0,1:T(8,128)S(1)}, u32[]{:S(2)}, u32[]{:S(2)}) collective-permute-start(f32[16,3,5377]{2,0,1:T(8,128)S(1)} %pad_maximum_fusion), channel_id=1, source_target_pairs={{0,1},{1,2},{2,3},{3,4},{4,5},{5,6},{6,7},{7,8},{8,9},{9,10},{10,1... | collective-permute-start | bytes 3097160 | tf_op jit(solution)/shard_map/ppermute | solution.py:271
  221.2 1.2 copy-start.4
  221.2 5.9 %copy-start = (f32[3,16,5376]{2,1,0:T(8,128)S(1)}, f32[3,16,5376]{2,1,0:T(8,128)}, u32[]{:S(2)}) copy-start(f32[3,16,5376]{2,1,0:T(8,128)} %get-tuple-element.15) | copy-start | bytes 3096580
  221.3 231.7 %copy-start.1 = (f32[5376]{0:T(1024)S(1)}, f32[5376]{0:T(1024)}, u32[]{:S(2)}) copy-start(f32[5376]{0:T(1024)} %param.19) | copy-start | bytes 64516
  222.4 4.7 collective-permute-start.1
  449.6 19.4 %slice-start = ((s8[5505024]{0:T(1024)(128)(4,1)}), s8[1310720]{0:T(1024)(128)(4,1)S(1)}, s32[]{:S(2)}) async-start(s8[5505024]{0:T(1024)(128)(4,1)} %bitcast.16), calls=%async_computation.1 | async-start | bytes 2621440
  453.5 15.4 %slice-start.1 = ((s8[5505024]{0:T(1024)(128)(4,1)}), s8[4194304]{0:T(1024)(128)(4,1)S(1)}, s32[]{:S(2)}) async-start(s8[5505024]{0:T(1024)(128)(4,1)} %bitcast.16), calls=%async_computation.2 | async-start | bytes 8388608
Sparse Core Ops, SparseCore 0:
  221.4 226.5 all-reduce.2

commit v3 on v2

--- a/solution.py
+++ b/solution.py
@@ -15,6 +15,9 @@
 LAG = 2
 SLOTS = LAG + 1
 ROWS = 8
+PART_SLOTS, RECV_SLOTS, OWN_SLOTS, EDGE_SLOTS = 6, 4, 8, 4
+STAGES = 8
+MESH = pl.DeviceIdType.MESH
 
 W0, BC, BA, BI, KL, KE = 0, 4, 5, 6, 7, 8
 N_PAR = 16
@@ -54,14 +57,102 @@
 
 def fused_kernel(n_dev, n_heads,
                  u_ref, gh_ref, halo_ref, mask_ref, wa_ref, wi_ref, wa2_ref, wi2_ref, par_ref, par2_ref,
-                 du_ref, tail_ref, back_ref, dwa_ref, dwi_ref, vec_ref,
+                 du_ref, grad_ref,
                  u_s, c_s, r_s, i_s, a_s, m_s, e_s, g_s, cb_s, h_scr, d_scr, ga_scr, gi_scr,
-                 send, recv, resp, carry, send_sem, recv_sem, give_sem, take_sem):
+                 send, recv, resp, carry, part, got0, got1, got2, got3, own, vec_all, vec_ref, du_s, tail_s, edge_out, edge_in,
+                 send_sem, recv_sem, give_sem, take_sem, sum_ssem, sum_rsem, edge_ssem, edge_rsem, du_sem, put_sem):
     n_batch, n_tok, width = u_ref.shape
     step_id = pl.program_id(0)
     me = lax.axis_index('cp')
     rows = 256
     span = rows // n_batch
+    n_items = n_heads + 1
+    core = lax.rem(me, 2)
+    x_at = lax.rem(me // 2, 2)
+    y_at = lax.rem(me // 4, 2)
+    z_at = me // 8
+    partner = me + 1 - 2 * core
+    x_peer = me + 2 - 4 * x_at
+    y_peer = me + 4 - 8 * y_at
+    bit1 = x_at + core * (y_at - x_at)
+    bit2 = y_at + core * (x_at - y_at)
+    peer1 = x_peer + core * (y_peer - x_peer)
+    peer2 = y_peer + core * (x_peer - y_peer)
+    half_rows, quarter_rows = width // 2, width // 4
+    piece = width // 16
+    base1 = bit1 * half_rows
+    base2 = base1 + bit2 * quarter_rows
+
+    def row_range(start, count):
+        return pl.ds(pl.multiple_of(start, count), count)
+
+    def sum_copies(stage, item):
+        p_at, r_at, o_at, s_at = (lax.rem(item, n) for n in (PART_SLOTS, RECV_SLOTS, OWN_SLOTS, OWN_SLOTS))
+
+        def one(index, src, dst, dev):
+            return pltpu.make_async_remote_copy(src_ref=src, dst_ref=dst, send_sem=sum_ssem.at[index, s_at],
+                                                recv_sem=sum_rsem.at[index, s_at], device_id=(dev,), device_id_type=MESH)
+
+        def z_peer(k):
+            z_to = lax.rem(z_at + k, 4)
+            return z_to, z_to * 8 + lax.rem(me, 8)
+
+        if stage == 0:
+            return [one(0, part.at[p_at, 1 - core], got0.at[r_at], partner)]
+        if stage == 1:
+            return [one(1, part.at[p_at, core, row_range((1 - bit1) * half_rows, half_rows)], got1.at[r_at], peer1)]
+        if stage == 2:
+            return [one(2, part.at[p_at, core, row_range(base1 + (1 - bit2) * quarter_rows, quarter_rows)], got2.at[r_at], peer2)]
+        if stage == 3:
+            return [one(2 + k, part.at[p_at, core, row_range(base2 + z_peer(k)[0] * piece, piece)], got3.at[r_at, k - 1], z_peer(k)[1])
+                    for k in (1, 2, 3)]
+        if stage == 4:
+            mine = own.at[o_at, row_range(base2 + z_at * piece, piece)]
+            return [one(5 + k, mine, mine, z_peer(k)[1]) for k in (1, 2, 3)]
+        if stage == 5:
+            mine = own.at[o_at, row_range(base2, quarter_rows)]
+            return [one(9, mine, mine, peer2)]
+        if stage == 6:
+            mine = own.at[o_at, row_range(base1, half_rows)]
+            return [one(10, mine, mine, peer1)]
+        return [one(11, own.at[o_at], grad_ref.at[core, item], partner)]
+
+    def put_copy(item):
+        slot = lax.rem(item, OWN_SLOTS)
+        return pltpu.make_async_copy(own.at[slot], grad_ref.at[core, item], put_sem.at[slot])
+
+    def sum_stage(stage, item):
+        p_at, r_at, o_at = (lax.rem(item, n) for n in (PART_SLOTS, RECV_SLOTS, OWN_SLOTS))
+        for copy in sum_copies(stage - 1, item):
+            copy.wait_recv()
+            copy.wait_send()
+        if stage == 1:
+            part[p_at, core] = part[p_at, core] + got0[r_at]
+        if stage == 2:
+            at = row_range(base1, half_rows)
+            part[p_at, core, at] = part[p_at, core, at] + got1[r_at]
+        if stage == 3:
+            at = row_range(base2, quarter_rows)
+            part[p_at, core, at] = part[p_at, core, at] + got2[r_at]
+        if stage == 4:
+            at = row_range(base2 + z_at * piece, piece)
+            own[o_at, at] = (part[p_at, core, at] + got3[r_at, 0]) + (got3[r_at, 1] + got3[r_at, 2])
+        if stage == STAGES:
+            put_copy(item).wait()
+        else:
+            for copy in sum_copies(stage, item):
+                copy.start()
+        if stage == STAGES - 1:
+            put_copy(item).start()
+
+    def edge_copy(head):
+        slot = lax.rem(head, EDGE_SLOTS)
+        return pltpu.make_async_remote_copy(src_ref=edge_out.at[slot], dst_ref=edge_in.at[slot], send_sem=edge_ssem.at[slot],
+                                            recv_sem=edge_rsem.at[slot], device_id=(lax.rem(me + n_dev - 1, n_dev),), device_id_type=MESH)
+
+    def du_copy(head):
+        slot = lax.rem(head, EDGE_SLOTS)
+        return pltpu.make_async_copy(du_s.at[slot], du_ref.at[:, :, pl.ds(pl.multiple_of(head * width, width), width)], du_sem.at[slot])
 
     def spread(src, dst, out_sem, in_sem, head, count):
         def one(k, _):
@@ -158,10 +249,34 @@
                 send.at[head][pl.ds(half * ROWS + row, n_batch, stride=2 * ROWS), :] = val
         spread(send, recv, send_sem, recv_sem, head, 3)
 
-    @pl.when(step_id >= LAG)
+    for stage in reversed(range(1, STAGES + 1)):
+        item_of = step_id - LAG - stage
+
+        @pl.when((item_of >= 0) & (item_of < n_items))
+        def _sum(stage=stage, item_of=item_of):
+            sum_stage(stage, item_of)
+
+    head_done = step_id - LAG - 2
+
+    @pl.when((head_done >= 0) & (head_done < n_heads))
+    def _stored():
+        du_copy(head_done).wait()
+
+    head_edge = step_id - LAG - 1
+
+    @pl.when((head_edge >= 0) & (head_edge < n_heads))
+    def _edge():
+        slot = lax.rem(head_edge, EDGE_SLOTS)
+        edge_copy(head_edge).wait_recv()
+        edge_copy(head_edge).wait_send()
+        du_s[slot, n_tok - HALO:] = (tail_s[slot] + edge_in[slot]).astype(jnp.bfloat16)
+        du_copy(head_edge).start()
+
+    @pl.when((step_id >= LAG) & (step_id < n_heads + LAG))
     def _second():
         head = step_id - LAG
         slot = lax.rem(step_id - LAG, SLOTS)
+        e_at = lax.rem(head, EDGE_SLOTS)
         settle(carry, take_sem, head, 2)
 
         for half in range(width // LANES):
@@ -203,17 +318,18 @@
 
             adj_in = carry.at[head][pl.ds(half * ROWS + 1, n_batch, stride=2 * ROWS), :]
             _, sum_a, sum_i, sum_l = lax.fori_loop(0, n_tok // STEPS, bwd_body, (adj_in, zero8, zero8, zero8))
-            vec_ref[0, GBA:GBA + 1, cols] = jnp.sum(sum_a, axis=0, keepdims=True)
-            vec_ref[0, GBI:GBI + 1, cols] = jnp.sum(sum_i, axis=0, keepdims=True)
-            vec_ref[0, GLAM:GLAM + 1, cols] = jnp.sum(sum_l, axis=0, keepdims=True)
+            vec_ref[GBA:GBA + 1, cols] = jnp.sum(sum_a, axis=0, keepdims=True)
+            vec_ref[GBI:GBI + 1, cols] = jnp.sum(sum_i, axis=0, keepdims=True)
+            vec_ref[GLAM:GLAM + 1, cols] = jnp.sum(sum_l, axis=0, keepdims=True)
 
         for start in range(0, n_tok, span):
             toks = slice(start, start + span)
             back = dot_nt(ga_scr[toks].reshape(rows, width), wa2_ref[0]) + dot_nt(gi_scr[toks].reshape(rows, width), wi2_ref[0])
             d_scr[toks] = d_scr[toks] + back.reshape(span, n_batch, width)
         all_c = cb_s[slot].reshape(n_tok * n_batch, width)
-        dwa_ref[0] = dot_tn(all_c, ga_scr[...].reshape(n_tok * n_batch, width))
-        dwi_ref[0] = dot_tn(all_c, gi_scr[...].reshape(n_tok * n_batch, width))
+        p_at = lax.rem(head, PART_SLOTS)
+        part[p_at, 0] = dot_tn(all_c, ga_scr[...].reshape(n_tok * n_batch, width))
+        part[p_at, 1] = dot_tn(all_c, gi_scr[...].reshape(n_tok * n_batch, width))
 
         for half in range(width // LANES):
             cols = slice(half * LANES, (half + 1) * LANES)
@@ -223,6 +339,7 @@
             def tap_body(chunk, run):
                 sums = list(run[:CONV + 1])
                 ahead = list(run[CONV + 1:])
+                last = [None] * HALO
                 base = n_tok - STEPS - chunk * STEPS
                 for step in reversed(range(STEPS)):
                     tok = base + step
@@ -232,19 +349,43 @@
                     for tap in range(CONV):
                         sums[tap] = sums[tap] + fold_rows(masked[tap] * u_s[slot, tok + HALO - tap, :, cols])
                     terms = [par2_ref[W0 + tap:W0 + tap + 1, cols] * masked[tap] for tap in range(CONV)]
-                    h_scr[tok, :, cols] = ahead[0] + terms[0]
+                    d_u = ahead[0] + terms[0]
+                    du_s[e_at, tok, :, cols] = d_u.astype(jnp.bfloat16)
+                    if step >= STEPS - HALO:
+                        last[step - STEPS + HALO] = d_u
                     ahead = [ahead[1] + terms[1], ahead[2] + terms[2], terms[3]]
-                return tuple(sums) + tuple(ahead)
-
-            out = lax.fori_loop(0, n_tok // STEPS, tap_body, (zero8,) * (CONV + 1) + (zero,) * HALO)
+                return tuple(sums) + tuple(ahead) + tuple(last)
+
+            def tap_loop(first, stop, run):
+                return lax.fori_loop(first, stop, lambda chunk, val: tap_body(chunk, val)[:-HALO], run)
+
+            begin = tap_body(0, (zero8,) * (CONV + 1) + (zero,) * HALO)
+            for row in range(HALO):
+                tail_s[e_at, row, :, cols] = begin[-HALO + row]
+            out = tap_loop(1, n_tok // STEPS, begin[:-HALO])
             for row in range(CONV + 1):
-                vec_ref[0, GW + row:GW + row + 1, cols] = jnp.sum(out[row], axis=0, keepdims=True)
+                vec_ref[GW + row:GW + row + 1, cols] = jnp.sum(out[row], axis=0, keepdims=True)
             for row in range(HALO):
-                back_ref[HALO - 1 - row, :, cols] = out[CONV + 1 + row]
-
-        tail_ref[...] = h_scr[n_tok - HALO:]
-        for start in range(0, n_tok, 16):
-            du_ref[:, start:start + 16, :] = jnp.swapaxes(h_scr[start:start + 16], 0, 1).astype(jnp.bfloat16)
+                edge_out[e_at, HALO - 1 - row, :, cols] = out[CONV + 1 + row]
+        edge_copy(head).start()
+        vec_all[pl.ds(pl.multiple_of(head * N_VEC, N_VEC), N_VEC), :] = vec_ref[...]
+
+    @pl.when(step_id == 0)
+    def _clear():
+        vec_all[...] = jnp.zeros_like(vec_all)
+
+    item_new = step_id - LAG
+
+    @pl.when(item_new == n_heads)
+    def _pack():
+        p_at = lax.rem(item_new, PART_SLOTS)
+        part[p_at, 0] = vec_all[...]
+        part[p_at, 1] = jnp.zeros_like(vec_all)
+
+    @pl.when((item_new >= 0) & (item_new < n_items))
+    def _share():
+        for copy in sum_copies(0, item_new):
+            copy.start()
 
     @pl.when(step_id == n_heads - 1 + LAG)
     def _drain():
@@ -258,7 +399,6 @@
 def solution(mesh):
     n_dev = mesh.shape['cp']
     to_next = [(src, src + 1) for src in range(n_dev - 1)]
-    to_prev = [(src + 1, src) for src in range(n_dev - 1)]
     seq_spec = P(None, 'cp', None)
     rep_spec = P()
 
@@ -286,7 +426,7 @@
             return jnp.minimum(step, n_heads - 1)
 
         def late(step):
-            return jnp.maximum(step - LAG, 0)
+            return jnp.clip(step - LAG, 0, n_heads - 1)
 
         def blk_row(at):
             return pl.BlockSpec((n_batch, n_tok, block_w), lambda s: (0, 0, at(s)))
@@ -307,35 +447,34 @@
         wire = pltpu.VMEM((n_heads, n_dev * ROWS, LANES), jnp.float32)
         sems = pltpu.SemaphoreType.DMA((n_heads,))
 
-        grad_u, tail, back, g_wa, g_wi, vecs = pl.pallas_call(
-            functools.partial(fused_kernel, n_dev, n_heads), grid=(n_heads + LAG,),
+        item_f32 = functools.partial(pltpu.VMEM, dtype=jnp.float32)
+        n_sems = 12
+        du_time, grads = pl.pallas_call(
+            functools.partial(fused_kernel, n_dev, n_heads), grid=(n_heads + 1 + LAG + STAGES,),
             in_specs=[blk_row(now), blk_row(now), blk_time(HALO, now), mask_spec, mat_spec(now), mat_spec(now),
                       mat_spec(late), mat_spec(late), par_spec(now), par_spec(late)],
-            out_specs=[blk_row(late), blk_time(HALO, late), blk_time(HALO, late), mat_spec(late), mat_spec(late),
-                       pl.BlockSpec((1, N_VEC, block_w), lambda s: (late(s), 0, 0))],
-            out_shape=[jax.ShapeDtypeStruct(u_in.shape, jnp.bfloat16), jax.ShapeDtypeStruct((HALO, n_batch, n_width), jnp.float32),
-                       jax.ShapeDtypeStruct((HALO, n_batch, n_width), jnp.float32),
-                       jax.ShapeDtypeStruct(a_gate_w.shape, jnp.float32), jax.ShapeDtypeStruct(a_gate_w.shape, jnp.float32),
-                       jax.ShapeDtypeStruct((n_heads, N_VEC, block_w), jnp.float32)],
+            out_specs=[pl.BlockSpec(memory_space=pl.ANY)] * 2,
+            out_shape=[jax.ShapeDtypeStruct((n_tok, n_batch, n_width), jnp.bfloat16),
+                       jax.ShapeDtypeStruct((2, n_heads + 1, block_w, block_w), jnp.float32)],
             scratch_shapes=[pltpu.VMEM((SLOTS, n_tok + HALO, n_batch, block_w), jnp.float32)] + [f32_slots] * 7
-            + [pltpu.VMEM((SLOTS, n_tok, n_batch, block_w), jnp.bfloat16), f32_scr, f32_scr, bf_scr, bf_scr]
-            + [wire] * 4 + [sems] * 4,
-            compiler_params=pltpu.CompilerParams(vmem_limit_bytes=63 * 2 ** 20, has_side_effects=True), name='fused_pass',
+            + [pltpu.VMEM((SLOTS, n_tok, n_batch, block_w), jnp.bfloat16), f32_scr, f32_scr, bf_scr, bf_scr] + [wire] * 4
+            + [item_f32((PART_SLOTS, 2, block_w, block_w)), item_f32((RECV_SLOTS, block_w, block_w)),
+               item_f32((RECV_SLOTS, block_w // 2, block_w)), item_f32((RECV_SLOTS, block_w // 4, block_w)),
+               item_f32((RECV_SLOTS, 3, block_w // 16, block_w)), item_f32((OWN_SLOTS, block_w, block_w)),
+               item_f32((block_w, block_w)), item_f32((N_VEC, block_w)),
+               pltpu.VMEM((EDGE_SLOTS, n_tok, n_batch, block_w), jnp.bfloat16)]
+            + [item_f32((EDGE_SLOTS, HALO, n_batch, block_w))] * 3
+            + [sems] * 4 + [pltpu.SemaphoreType.DMA((n_sems, OWN_SLOTS))] * 2
+            + [pltpu.SemaphoreType.DMA((EDGE_SLOTS,))] * 3 + [pltpu.SemaphoreType.DMA((OWN_SLOTS,))],
+            compiler_params=pltpu.CompilerParams(vmem_limit_bytes=67043328, has_side_effects=True), name='fused_pass',
         )(u_in, grad_h, halo_u, masks, a_gate_w, x_gate_w, a_gate_w, x_gate_w, par, par)
-        halo_back = lax.ppermute(back, 'cp', to_prev)
-        return grad_u, tail, halo_back, g_wa, g_wi, vecs
-
-    def full_fn(*args):
-        lam_param = args[-1]
-        grad_u, tail, halo_back, g_wa, g_wi, vecs = local_fn(*args)
-        tail = jnp.swapaxes((tail + halo_back).astype(jnp.bfloat16), 0, 1)
-        grad_u = lax.dynamic_update_slice(grad_u, tail, (0, grad_u.shape[1] - HALO, 0))
-        g_wa, g_wi, vecs = lax.psum((g_wa, g_wi, vecs), 'cp')
-        vecs = jnp.swapaxes(vecs, 0, 1).reshape(N_VEC, -1)
+        vecs = grads[0, n_heads, :n_heads * N_VEC].reshape(n_heads, N_VEC, block_w)
+        vecs = jnp.swapaxes(vecs, 0, 1).reshape(N_VEC, n_width)
         g_lam = 8.0 * jax.nn.sigmoid(-lam_param) * vecs[GLAM]
-        return (grad_u, vecs[GW:GW + CONV], vecs[GBC], g_wa, vecs[GBA], g_wi, vecs[GBI], g_lam)
-
-    return jax.shard_map(full_fn, mesh=mesh,
+        return (jnp.swapaxes(du_time, 0, 1), vecs[GW:GW + CONV], vecs[GBC], grads[0, :n_heads], vecs[GBA],
+                grads[1, :n_heads], vecs[GBI], g_lam)
+
+    return jax.shard_map(local_fn, mesh=mesh,
                          in_specs=(seq_spec, P(None, 'cp'), seq_spec, rep_spec, rep_spec, rep_spec,
                                    rep_spec, rep_spec, rep_spec, rep_spec),
                          out_specs=(seq_spec,) + (rep_spec,) * 7, check_vma=False)

time: 479 us -> 281 us (0.59)
  waiting for transfers between devices: 214 us -> 0.01 us
  Pallas kernels: 201 us -> 242 us
  between operations: 14.2 us -> 0.85 us
  local copies, waits for them, and re-layouts: 42.7 us -> 32.8 us
    psum x1 -> x0, waiting for transfers between devices: 211 us -> none  [full_fn(): g_wa, g_wi, vecs = lax.psum((g_wa, g_wi, vecs), 'cp')]
    pallas_call x1, Pallas kernels: 201 us -> 242 us  [local_fn(): pl.pallas_call(functools.partial(fused_kernel, n_dev, n_heads), grid=(n_h...]
    squeeze x4 -> x5, local copies, waits for them, and re-layouts: 1.83 us -> 11.7 us  [the longest x1 9.91 us: local_fn(): grads[1, :n_heads]]
    dynamic_update_slice x1 -> x0, local copies, waits for them, and re-layouts: 9.66 us -> none  [full_fn(): lax.dynamic_update_slice(grad_u, tail, (0, grad_u.shape[1] - HALO, 0))]
    unnamed x18 -> x16, local copies, waits for them, and re-layouts: 19.1 us -> 11.2 us
  transfers between devices with their start and end apart: 3 -> 1, of which waited for: 2 -> 0; matrix products, arithmetic and copies ran while one was open for 3% -> 2% of each run, Pallas kernels for 0% -> 0%
where the time goes in v3:
time: 281 us
  Pallas kernels  242 us (86%)
  local copies, waits for them, and re-layouts  32.8 us (12%)
    pallas_call x1, Pallas kernels, local_fn(): pl.pallas_call(functools.partial(fused_kernel, n_dev, n_heads), grid=(n_h...  242 us
    unnamed x16, local copies, waits for them, and re-layouts  11.2 us
    squeeze x1, local copies, waits for them, and re-layouts, local_fn(): grads[1, :n_heads]  9.91 us
  transfers between devices with their start and end apart: 1, of which 0 were waited for; matrix products, arithmetic and copies ran while one was open for 2% of the time, Pallas kernels for 0%

profile of v3, /device:TPU:0, one launch (start us, length us, event | category | flops | bytes accessed | tf_op | source)
XLA Modules:
  0.0 280.9 jit_solution(15446653793757714646)
XLA Ops:
  0.7 0.8 slice_convert_fusion.1
  1.5 0.1 copy.50
  1.6 0.1 copy.41
  1.7 1.7 slice.66
  3.4 0.1 copy_convert_fusion
  3.4 0.1 pad_maximum_fusion
  3.5 2.5 collective-permute-start
  6.0 0.8 broadcast_in_dim.13
  6.8 0.8 broadcast_in_dim.28
  7.5 0.8 broadcast_in_dim.29
  8.3 0.8 broadcast_multiply_fusion
  9.1 1.5 concatenate.11.par_ref.par2_ref
  10.7 0.1 fusion.7
  10.8 0.2 copy.46
  11.0 0.1 add_bitcast_fusion
  11.1 0.1 fusion.1
  11.2 0.1 copy.43
  11.3 1.0 slice_bitcast_fusion.2.halo_ref
  12.3 1.6 broadcast_in_dim.12.mask_ref
  13.9 242.2 %fused_pass.1 = (bf16[64,16,5376]{2,1,0:T(8,128)(2,1)}, f32[2,22,256,256]{3,2,1,0:T(8,128)}) custom-call(bf16[16,64,5376]{2,1,0:T(8,128)(2,1)} %u_ref.1, f32[16,64,5376]{2,1,0:T(8,128)} %gh_ref.1, f32[3,16,5376]{2,1,0:T(8,128)} %slice_bitcast_fusion.2.halo_ref, f32[3,64,16,128]{3,2,1,0:T(8,128)} %broadcast_in_dim.12.mask_ref, bf16[21,256,256]{2,1,0:T(8,128)(2,1)} %wa2_ref.1, ...), custom_call_target="tpu_custom_call" | custom-call | tf_op jit(solution)/shard_map/fused_pass/pallas_call | solution.py:452
  256.2 0.0 slice-start
  256.2 1.1 slice_bitcast_fusion.3
  257.3 0.0 slice-start.1
  257.3 9.9 %slice_bitcast_fusion = (f32[21,256,256]{2,1,0:T(8,128)}, f32[21,256,256]{2,1,0:T(8,128)}) fusion(f32[2,22,256,256]{3,2,1,0:T(8,128)} %get-tuple-element.11), kind=kLoop, calls=%fused_computation | loop fusion | bytes 22020096 | tf_op jit(solution)/shard_map/squeeze | solution.py:475
  267.2 0.1 copy.53
  267.3 0.0 copy-start
  267.3 10.4 %copy.45 = bf16[16,64,5376]{2,1,0:T(8,128)(2,1)} copy(bf16[16,64,5376]{2,0,1:T(8,128)(2,1)S(1)} %bitcast.27) | data formatting | bytes 22020096
  277.8 0.7 copy.49
  278.4 0.6 multiply_multiply_fusion
  279.1 0.6 squeeze.23
  279.7 0.6 squeeze.21
  280.3 0.6 squeeze.19
  (20 shorter events, 0.1 us)
Async XLA Ops:
  0.6 10.4 %copy-start.2 = (s32[16,64]{1,0:T(8,128)S(1)}, s32[16,64]{1,0:T(8,128)}, u32[]{:S(2)}) copy-start(s32[16,64]{1,0:T(8,128)} %param.11) | copy-start | bytes 12292
  0.6 8.5 %copy-start.1 = (f32[4,5376]{1,0:T(4,128)S(1)}, f32[4,5376]{1,0:T(4,128)}, u32[]{:S(2)}) copy-start(f32[4,5376]{1,0:T(4,128)} %param.13) | copy-start | bytes 258052
  3.5 7.3 %collective-permute-start = (f32[16,3,5377]{2,0,1:T(8,128)S(1)}, f32[16,3,5377]{2,0,1:T(8,128)S(1)}, u32[]{:S(2)}, u32[]{:S(2)}) collective-permute-start(f32[16,3,5377]{2,0,1:T(8,128)S(1)} %pad_maximum_fusion), channel_id=1, source_target_pairs={{0,1},{1,2},{2,3},{3,4},{4,5},{5,6},{6,7},{7,8},{8,9},{9,10},{10,1... | collective-permute-start | bytes 3097160 | tf_op jit(solution)/shard_map/ppermute | solution.py:411
  256.2 11.1 %slice-start = ((s8[11010048]{0:T(1024)(128)(4,1)}), s8[4194304]{0:T(1024)(128)(4,1)S(1)}, s32[]{:S(2)}) async-start(s8[11010048]{0:T(1024)(128)(4,1)} %bitcast.25), calls=%async_computation | async-start | bytes 8388608
  257.3 10.0 %slice-start.1 = ((s8[11010048]{0:T(1024)(128)(4,1)}), s8[4194304]{0:T(1024)(128)(4,1)S(1)}, s32[]{:S(2)}) async-start(s8[11010048]{0:T(1024)(128)(4,1)} %bitcast.25), calls=%async_computation.1 | async-start | bytes 8388608
  257.3 10.0 %slice-start.2 = ((s8[11010048]{0:T(1024)(128)(4,1)}), s8[2621440]{0:T(1024)(128)(4,1)S(1)}, s32[]{:S(2)}) async-start(s8[11010048]{0:T(1024)(128)(4,1)} %bitcast.25), calls=%async_computation.2 | async-start | bytes 5242880
  267.3 11.1 %copy-start = (f32[5376]{0:T(1024)S(1)}, f32[5376]{0:T(1024)}, u32[]{:S(2)}) copy-start(f32[5376]{0:T(1024)} %param.19) | copy-start | bytes 64516

commit v4 on v3

v4 whole, which is shorter than its diff:
```python
import functools

import jax
import jax.numpy as jnp
from jax import lax
from jax.experimental import pallas as pl
from jax.experimental.pallas import tpu as pltpu
from jax.sharding import PartitionSpec as P

CONV = 4
HALO = CONV - 1
LOG2E = 1.4426950408889634
LN2 = 0.6931471805599453
START_BIAS = -1e4
LANES = 128
STEPS = 16
BLOCK = 16
LAG = 3
SLOTS = LAG + 1
GROUP, DEPTH = 8, 4
SUM_ROWS, IN_ROWS = 12, 8
PITCH = 16
PART_SLOTS, RECV_SLOTS, OWN_SLOTS, EDGE_SLOTS, EDGE_IN = 6, 4, 8, 4, 8
STAGES, FIRST_SLOTS = 8, 4
AFTER = (0, 1, 2, 3, 4, 5, 6, 7, 8)
MESH = pl.DeviceIdType.MESH

W0, BC, BA, BI, KL, KE = 0, 4, 5, 6, 7, 8
N_PAR = 16
GW, GBC, GBA, GBI, GLAM = 0, 4, 5, 6, 7
N_VEC = 8


def sigmoid_of(pre):
    root = lax.rsqrt(1.0 + jnp.exp2(pre * (-LOG2E)))
    return root * root


def decay_of(gate_r, par_ke, bias):
    log_two = gate_r * par_ke + bias
    decay = jnp.exp2(log_two)
    square = decay * decay
    gap = jnp.tanh(log_two * (-LN2)) * (1.0 + square)
    inv_root = lax.rsqrt(gap)
    return decay, gap * inv_root, square * inv_root * inv_root


def fold_rows(arr):
    return arr[:8] + arr[8:]


def dot_nn(lhs, rhs):
    return lax.dot_general(lhs, rhs, (((1,), (0,)), ((), ())), preferred_element_type=jnp.float32)


def dot_nt(lhs, rhs):
    return lax.dot_general(lhs, rhs, (((1,), (1,)), ((), ())), preferred_element_type=jnp.float32)


def dot_tn(lhs, rhs):
    return lax.dot_general(lhs, rhs, (((0,), (0,)), ((), ())), preferred_element_type=jnp.float32)


def fused_kernel(n_dev, n_heads,
                 u_ref, tail_ref, gh_ref, mask_ref, wa_ref, wi_ref, wa2_ref, wi2_ref, par_ref, par2_ref,
                 du_ref, grad_ref,
                 u_s, c_s, r_s, i_s, a_s, m_s, e_s, g_s, cb_s, h_scr, d_scr, ga_scr, gi_scr,
                 send, recv, group, resp, carry, halo_out, halo_in, part, got0, got1, got2, got3, own, vec_all, vec_ref, du_s, tail_s, edge_out, edge_in,
                 send_sem, recv_sem, group_ssem, group_rsem, give_sem, take_sem, halo_ssem, halo_rsem, sum_ssem, sum_rsem, edge_ssem, edge_rsem, du_sem, put_sem):
    n_batch, n_tok, width = u_ref.shape
    step_id = pl.program_id(0)
    me = lax.axis_index('cp')
    rows = 256
    core = lax.rem(me, 2)
    x_at = lax.rem(me // 2, 2)
    y_at = lax.rem(me // 4, 2)
    z_at = me // GROUP
    place = lax.rem(me, GROUP)
    partner = me + 1 - 2 * core
    x_peer = me + 2 - 4 * x_at
    y_peer = me + 4 - 8 * y_at
    bit1 = x_at + core * (y_at - x_at)
    bit2 = y_at + core * (x_at - y_at)
    peer1 = x_peer + core * (y_peer - x_peer)
    peer2 = y_peer + core * (x_peer - y_peer)
    half_rows, quarter_rows = width // 2, width // 4
    piece = width // 16
    base1 = bit1 * half_rows
    base2 = base1 + bit2 * quarter_rows

    def row_range(start, count):
        return pl.ds(pl.multiple_of(start, count), count)

    def sum_copies(stage, item):
        p_at, r_at, o_at, s_at, f_at = (lax.rem(item, n) for n in (PART_SLOTS, RECV_SLOTS, OWN_SLOTS, OWN_SLOTS, FIRST_SLOTS))

        def one(index, src, dst, dev):
            return pltpu.make_async_remote_copy(src_ref=src, dst_ref=dst, send_sem=sum_ssem.at[index, s_at],
                                                recv_sem=sum_rsem.at[index, s_at], device_id=(dev,), device_id_type=MESH)

        def z_peer(k):
            z_to = lax.rem(z_at + k, 4)
            return z_to, z_to * GROUP + place

        if stage == 0:
            return [one(0, part.at[p_at, 1 - core], got0.at[f_at], partner)]
        if stage == 1:
            return [one(1, part.at[p_at, core, row_range((1 - bit1) * half_rows, half_rows)], got1.at[r_at], peer1)]
        if stage == 2:
            return [one(2, part.at[p_at, core, row_range(base1 + (1 - bit2) * quarter_rows, quarter_rows)], got2.at[r_at], peer2)]
        if stage == 3:
            return [one(2 + k, part.at[p_at, core, row_range(base2 + z_peer(k)[0] * piece, piece)], got3.at[r_at, k - 1], z_peer(k)[1])
                    for k in (1, 2, 3)]
        if stage == 4:
            mine = own.at[o_at, row_range(base2 + z_at * piece, piece)]
            return [one(5 + k, mine, mine, z_peer(k)[1]) for k in (1, 2, 3)]
        if stage == 5:
            mine = own.at[o_at, row_range(base2, quarter_rows)]
            return [one(9, mine, mine, peer2)]
        if stage == 6:
            mine = own.at[o_at, row_range(base1, half_rows)]
            return [one(10, mine, mine, peer1)]
        return [one(11, own.at[o_at], grad_ref.at[core, item], partner)]

    def put_copy(item):
        slot = lax.rem(item, OWN_SLOTS)
        return pltpu.make_async_copy(own.at[slot], grad_ref.at[core, item], put_sem.at[slot])

    def sum_stage(stage, item):
        p_at, r_at, o_at = (lax.rem(item, n) for n in (PART_SLOTS, RECV_SLOTS, OWN_SLOTS))
        for copy in sum_copies(stage - 1, item):
            copy.wait_recv()
            copy.wait_send()
        if stage == 1:
            part[p_at, core] = part[p_at, core] + got0[lax.rem(item, FIRST_SLOTS)]
        if stage == 2:
            at = row_range(base1, half_rows)
            part[p_at, core, at] = part[p_at, core, at] + got1[r_at]
        if stage == 3:
            at = row_range(base2, quarter_rows)
            part[p_at, core, at] = part[p_at, core, at] + got2[r_at]
        if stage == 4:
            at = row_range(base2 + z_at * piece, piece)
            own[o_at, at] = (part[p_at, core, at] + got3[r_at, 0]) + (got3[r_at, 1] + got3[r_at, 2])
        if stage == STAGES:
            put_copy(item).wait()
        else:
            for copy in sum_copies(stage, item):
                copy.start()
        if stage == STAGES - 1:
            put_copy(item).start()

    def edge_copy(head):
        slot, to = lax.rem(head, EDGE_SLOTS), lax.rem(head, EDGE_IN)
        return pltpu.make_async_remote_copy(src_ref=edge_out.at[slot], dst_ref=edge_in.at[to], send_sem=edge_ssem.at[slot],
                                            recv_sem=edge_rsem.at[to], device_id=(lax.rem(me + n_dev - 1, n_dev),), device_id_type=MESH)

    def du_copy(head):
        slot = lax.rem(head, EDGE_SLOTS)
        return pltpu.make_async_copy(du_s.at[slot], du_ref.at[:, :, pl.ds(pl.multiple_of(head * width, width), width)], du_sem.at[slot])

    def block_of(index, pitch, count):
        return pl.ds(pl.multiple_of(index * pitch, pitch), count)

    def spread(src, dst, out_sem, in_sem, head, pitch, count):
        def one(k, _):
            to = lax.rem(place + k, GROUP)
            pltpu.make_async_remote_copy(
                src_ref=src.at[head, block_of(to, pitch, count)], dst_ref=dst.at[head, block_of(place, pitch, count)],
                send_sem=out_sem.at[head], recv_sem=in_sem.at[head],
                device_id=(z_at * GROUP + to,), device_id_type=MESH).start()
            return 0
        lax.fori_loop(1, GROUP, one, 0, unroll=True)
        own_rows = block_of(place, pitch, pitch)
        dst[head, own_rows, :] = src[head, own_rows, :]

    def settle(buf, sem, head, total):
        all_rows = buf.at[head, pl.ds(0, total)]
        pltpu.make_async_copy(all_rows, all_rows, sem.at[head]).wait()

    def rows_of(buf, head, index, quantity):
        start = index * PITCH + 4 * quantity
        return buf[head, start:start + 4, :]

    def halo_copy(head):
        slot = lax.rem(head, EDGE_SLOTS)
        return pltpu.make_async_remote_copy(src_ref=halo_out.at[slot], dst_ref=halo_in.at[slot], send_sem=halo_ssem.at[slot],
                                            recv_sem=halo_rsem.at[slot], device_id=(lax.rem(me + 1, n_dev),), device_id_type=MESH)

    def halo_send(head, src_ref):
        last = jnp.swapaxes(src_ref[:, src_ref.shape[1] - BLOCK:, :].astype(jnp.float32), 0, 1)
        halo_out[lax.rem(head, EDGE_SLOTS)] = last[BLOCK - HALO:]
        halo_copy(head).start()

    @pl.when(step_id == 0)
    def _begin():
        vec_all[...] = jnp.zeros_like(vec_all)
        halo_send(0, u_ref)

    def group_copies(head):
        mine = group.at[head, block_of(z_at, PITCH, SUM_ROWS)]
        return [pltpu.make_async_remote_copy(src_ref=mine, dst_ref=mine, send_sem=group_ssem.at[k, head], recv_sem=group_rsem.at[k, head],
                                             device_id=(lax.rem(z_at + 1 + k, DEPTH) * GROUP + place,), device_id_type=MESH)
                for k in range(DEPTH - 1)]

    def combine(head):
        for copy in group_copies(head):
            copy.wait_recv()
            copy.wait_send()
        state = jnp.zeros((4, LANES), jnp.float32)
        adj = jnp.zeros((4, LANES), jnp.float32)
        for index in range(DEPTH - 1):
            step_state = rows_of(group, head, index, 0) * state + rows_of(group, head, index, 1)
            state = jnp.where(index < z_at, step_state, state)
            other = DEPTH - 1 - index
            step_adj = rows_of(group, head, other, 0) * adj + rows_of(group, head, other, 2)
            adj = jnp.where(other > z_at, step_adj, adj)
        for index in range(GROUP):
            other = GROUP - 1 - index
            resp[head, index * IN_ROWS:index * IN_ROWS + 4, :] = state
            resp[head, other * IN_ROWS + 4:other * IN_ROWS + 8, :] = adj
            state = rows_of(recv, head, index, 0) * state + rows_of(recv, head, index, 1)
            adj = rows_of(recv, head, other, 0) * adj + rows_of(recv, head, other, 2)
        spread(resp, carry, give_sem, take_sem, head, IN_ROWS, IN_ROWS)

    def put_rows(head, quantity, half, val):
        for high in range(2):
            send.at[head][pl.ds(4 * quantity + 2 * high + half, GROUP, stride=PITCH), :] = val[high * GROUP:(high + 1) * GROUP]

    def take_rows(head, quantity, half):
        return jnp.concatenate([carry.at[head][pl.ds(4 * quantity + 2 * high + half, GROUP, stride=IN_ROWS), :] for high in range(2)], axis=0)

    @pl.when(step_id < n_heads)
    def _first():
        head = step_id
        slot = lax.rem(step_id, SLOTS)
        halo_copy(head).wait_recv()
        halo_copy(head).wait_send()
        u_s[slot, :HALO] = halo_in[lax.rem(head, EDGE_SLOTS)]

        @pl.when(head + 1 < n_heads)
        def _next_halo():
            halo_send(head + 1, tail_ref)

        for start in range(0, n_tok, BLOCK):
            u_s[slot, HALO + start:HALO + start + BLOCK] = jnp.swapaxes(u_ref[:, start:start + BLOCK, :].astype(jnp.float32), 0, 1)
            for tok in range(start, start + BLOCK):
                for lane in range(0, width, LANES):
                    cols = slice(lane, lane + LANES)
                    acc = par_ref[BC:BC + 1, cols] + par_ref[W0:W0 + 1, cols] * u_s[slot, tok + HALO, :, cols]
                    for tap in range(1, CONV):
                        acc = acc + par_ref[W0 + tap:W0 + tap + 1, cols] * (mask_ref[tap - 1, tok] * u_s[slot, tok + HALO - tap, :, cols])
                    c_s[slot, tok, :, cols] = acc
                    cb_s[slot, tok, :, cols] = acc.astype(jnp.bfloat16)
            g_s[slot, start:start + BLOCK] = jnp.swapaxes(gh_ref[:, start:start + BLOCK, :], 0, 1)
            part_c = cb_s[slot, start:start + BLOCK].reshape(rows, width)
            r_s[slot, start:start + BLOCK] = dot_nn(part_c, wa_ref[0]).reshape(BLOCK, n_batch, width)
            i_s[slot, start:start + BLOCK] = dot_nn(part_c, wi_ref[0]).reshape(BLOCK, n_batch, width)

        for half in range(width // LANES):
            cols = slice(half * LANES, (half + 1) * LANES)

            def fwd_body(chunk, run):
                state, prod = run
                base = chunk * STEPS
                for step in range(STEPS):
                    tok = base + step
                    gate_r = sigmoid_of(r_s[slot, tok, :, cols] + par_ref[BA:BA + 1, cols])
                    gate_i = sigmoid_of(i_s[slot, tok, :, cols] + par_ref[BI:BI + 1, cols])
                    decay, mult, ratio = decay_of(gate_r, par_ref[KE:KE + 1, cols], mask_ref[HALO, tok])
                    r_s[slot, tok, :, cols] = gate_r
                    i_s[slot, tok, :, cols] = gate_i
                    a_s[slot, tok, :, cols] = decay
                    m_s[slot, tok, :, cols] = mult
                    e_s[slot, tok, :, cols] = ratio
                    state = decay * state + mult * (gate_i * c_s[slot, tok, :, cols])
                    prod = decay * prod
                return state, prod

            zero = jnp.zeros((n_batch, LANES), jnp.float32)
            state, prod = lax.fori_loop(0, n_tok // STEPS, fwd_body, (zero, zero + 1.0))

            put_rows(head, 0, half, prod)
            put_rows(head, 1, half, state)

        def adj_body(chunk, adj):
            base = n_tok - STEPS - chunk * STEPS
            for step in reversed(range(STEPS)):
                tok = base + step
                adj = a_s[slot, tok] * (g_s[slot, tok] + adj)
            return adj

        first = lax.fori_loop(0, n_tok // STEPS, adj_body, jnp.zeros((n_batch, width), jnp.float32))
        for half in range(width // LANES):
            put_rows(head, 2, half, first[:, half * LANES:(half + 1) * LANES])
        spread(send, recv, send_sem, recv_sem, head, PITCH, SUM_ROWS)

    @pl.when((step_id >= 2) & (step_id <= n_heads + 1))
    def _combine():
        combine(step_id - 2)

    @pl.when((step_id >= 1) & (step_id <= n_heads))
    def _group():
        head = step_id - 1
        settle(recv, recv_sem, head, (GROUP - 1) * SUM_ROWS)
        prod = jnp.ones((4, LANES), jnp.float32)
        state = jnp.zeros((4, LANES), jnp.float32)
        adj = jnp.zeros((4, LANES), jnp.float32)
        for index in range(GROUP):
            decay = rows_of(recv, head, index, 0)
            state = decay * state + rows_of(recv, head, index, 1)
            prod = decay * prod
            other = GROUP - 1 - index
            adj = rows_of(recv, head, other, 0) * adj + rows_of(recv, head, other, 2)
        mine = block_of(z_at, PITCH, PITCH)
        group[head, mine, :] = jnp.concatenate([prod, state, adj, jnp.zeros_like(adj)], axis=0)
        for copy in group_copies(head):
            copy.start()

    for stage in reversed(range(1, STAGES + 1)):
        item_of = step_id - LAG - AFTER[stage]

        @pl.when((item_of >= 0) & (item_of < n_heads))
        def _sum(stage=stage, item_of=item_of):
            sum_stage(stage, item_of)

        @pl.when(item_of == n_heads - 1)
        def _sum_vectors(stage=stage):
            sum_stage(stage, n_heads)

    head_done = step_id - LAG - 3

    @pl.when((head_done >= 0) & (head_done < n_heads))
    def _stored():
        du_copy(head_done).wait()

    head_edge = step_id - LAG - 2

    @pl.when((head_edge >= 0) & (head_edge < n_heads))
    def _edge():
        slot = lax.rem(head_edge, EDGE_SLOTS)
        edge_copy(head_edge).wait_recv()
        edge_copy(head_edge).wait_send()
        du_s[slot, n_tok - HALO:] = (tail_s[slot] + edge_in[lax.rem(head_edge, EDGE_IN)]).astype(jnp.bfloat16)
        du_copy(head_edge).start()

    @pl.when((step_id >= LAG) & (step_id < n_heads + LAG))
    def _second():
        head = step_id - LAG
        slot = lax.rem(step_id - LAG, SLOTS)
        e_at = lax.rem(head, EDGE_SLOTS)
        settle(carry, take_sem, head, (GROUP - 1) * IN_ROWS)

        def state_body(chunk, state):
            base = chunk * STEPS
            for step in range(STEPS):
                tok = base + step
                h_scr[tok] = state
                state = a_s[slot, tok] * state + m_s[slot, tok] * (i_s[slot, tok] * c_s[slot, tok])
            return state

        state_in = [take_rows(head, 0, half) for half in range(width // LANES)]
        lax.fori_loop(0, n_tok // STEPS, state_body, jnp.concatenate(state_in, axis=1))

        for half in range(width // LANES):
            cols = slice(half * LANES, (half + 1) * LANES)
            zero8 = jnp.zeros((8, LANES), jnp.float32)

            def bwd_body(chunk, run):
                adj_next, sum_a, sum_i, sum_l = run
                base = n_tok - STEPS - chunk * STEPS
                for step in reversed(range(STEPS)):
                    tok = base + step
                    gate_r = r_s[slot, tok, :, cols]
                    gate_i = i_s[slot, tok, :, cols]
                    conv_c = c_s[slot, tok, :, cols]
                    adj = g_s[slot, tok, :, cols] + adj_next
                    adj_next = a_s[slot, tok, :, cols] * adj
                    direct = adj * m_s[slot, tok, :, cols] * gate_i
                    d_input = direct * conv_c
                    d_pre_i = d_input * (1.0 - gate_i)
                    d_log = adj_next * h_scr[tok, :, cols] - d_input * e_s[slot, tok, :, cols]
                    d_log_r = d_log * gate_r
                    d_pre_a = d_log_r * (par2_ref[KL:KL + 1, cols] * (1.0 - gate_r))
                    sum_l = sum_l + fold_rows(d_log_r)
                    sum_a = sum_a + fold_rows(d_pre_a)
                    sum_i = sum_i + fold_rows(d_pre_i)
                    d_scr[tok, :, cols] = direct
                    ga_scr[tok, :, cols] = d_pre_a.astype(jnp.bfloat16)
                    gi_scr[tok, :, cols] = d_pre_i.astype(jnp.bfloat16)
                return adj_next, sum_a, sum_i, sum_l

            adj_in = take_rows(head, 1, half)
            _, sum_a, sum_i, sum_l = lax.fori_loop(0, n_tok // STEPS, bwd_body, (adj_in, zero8, zero8, zero8))
            vec_ref[GBA:GBA + 1, cols] = jnp.sum(sum_a, axis=0, keepdims=True)
            vec_ref[GBI:GBI + 1, cols] = jnp.sum(sum_i, axis=0, keepdims=True)
            vec_ref[GLAM:GLAM + 1, cols] = jnp.sum(sum_l, axis=0, keepdims=True)

        p_at = lax.rem(head, PART_SLOTS)
        all_c = cb_s[slot].reshape(n_tok * n_batch, width)
        part[p_at, 0] = dot_tn(all_c, ga_scr[...].reshape(n_tok * n_batch, width))
        part[p_at, 1] = dot_tn(all_c, gi_scr[...].reshape(n_tok * n_batch, width))

        halves = width // LANES
        sums = [[jnp.zeros((8, LANES), jnp.float32)] * (CONV + 1) for _ in range(halves)]
        ahead = [[jnp.zeros((n_batch, LANES), jnp.float32)] * HALO for _ in range(halves)]
        for start in reversed(range(0, n_tok, BLOCK)):
            toks = slice(start, start + BLOCK)
            back = dot_nt(ga_scr[toks].reshape(rows, width), wa2_ref[0]) + dot_nt(gi_scr[toks].reshape(rows, width), wi2_ref[0])
            d_scr[toks] = d_scr[toks] + back.reshape(BLOCK, n_batch, width)
            for half in range(halves):
                cols = slice(half * LANES, (half + 1) * LANES)
                tot, nxt = sums[half], ahead[half]
                for tok in reversed(range(start, start + BLOCK)):
                    d_conv = d_scr[tok, :, cols]
                    tot[CONV] = tot[CONV] + fold_rows(d_conv)
                    masked = [d_conv] + [mask_ref[tap - 1, tok] * d_conv for tap in range(1, CONV)]
                    for tap in range(CONV):
                        tot[tap] = tot[tap] + fold_rows(masked[tap] * u_s[slot, tok + HALO - tap, :, cols])
                    terms = [par2_ref[W0 + tap:W0 + tap + 1, cols] * masked[tap] for tap in range(CONV)]
                    d_u = nxt[0] + terms[0]
                    du_s[e_at, tok, :, cols] = d_u.astype(jnp.bfloat16)
                    if tok >= n_tok - HALO:
                        tail_s[e_at, tok - n_tok + HALO, :, cols] = d_u
                    nxt = [nxt[1] + terms[1], nxt[2] + terms[2], terms[3]]
                ahead[half] = nxt
        for half in range(halves):
            cols = slice(half * LANES, (half + 1) * LANES)
            for row in range(CONV + 1):
                vec_ref[GW + row:GW + row + 1, cols] = jnp.sum(sums[half][row], axis=0, keepdims=True)
            for row in range(HALO):
                edge_out[e_at, HALO - 1 - row, :, cols] = ahead[half][row]
        edge_copy(head).start()
        vec_all[pl.ds(pl.multiple_of(head * N_VEC, N_VEC), N_VEC), :] = vec_ref[...]

    item_new = step_id - LAG

    @pl.when((item_new >= 0) & (item_new < n_heads))
    def _share():
        for copy in sum_copies(0, item_new):
            copy.start()

    @pl.when(item_new == n_heads - 1)
    def _share_vectors():
        p_at = n_heads % PART_SLOTS
        part[p_at, 0] = vec_all[...]
        part[p_at, 1] = jnp.zeros_like(vec_all)
        for copy in sum_copies(0, n_heads):
            copy.start()

    @pl.when(step_id == n_heads - 1 + LAG)
    def _drain():
        def one(head, _):
            settle(send, send_sem, head, (GROUP - 1) * SUM_ROWS)
            settle(resp, give_sem, head, (GROUP - 1) * IN_ROWS)
            return 0
        lax.fori_loop(0, n_heads, one, 0)


def solution(mesh):
    n_dev = mesh.shape['cp']
    to_next = [(src, src + 1) for src in range(n_dev - 1)]
    seq_spec = P(None, 'cp', None)
    rep_spec = P()

    def local_fn(u_in, seg_ids, grad_h, conv_w, conv_b, a_gate_w, a_gate_b, x_gate_w, x_gate_b, lam_param):
        n_batch, n_tok, n_width = u_in.shape
        n_heads, block_w, _ = a_gate_w.shape
        has_prev = lax.axis_index('cp') > 0
        halo_seg = lax.ppermute(seg_ids[:, n_tok - HALO:], 'cp', to_next)
        seg_ext = jnp.concatenate([halo_seg, seg_ids], axis=1).T
        ext_ok = (jnp.arange(n_tok + HALO) >= HALO) | has_prev
        masks = []
        for tap in range(1, CONV):
            tap_ok = (seg_ext[HALO - tap:HALO - tap + n_tok] == seg_ext[HALO:]) & ext_ok[HALO - tap:HALO - tap + n_tok, None]
            masks.append(tap_ok.astype(jnp.float32))
        masks.append((1.0 - masks[0]) * START_BIAS)
        masks = jnp.broadcast_to(jnp.stack(masks)[..., None], (HALO + 1, n_tok, n_batch, LANES))
        log_rate = -8.0 * jax.nn.softplus(-lam_param)
        par = jnp.concatenate([conv_w, conv_b[None], a_gate_b[None], x_gate_b[None], log_rate[None], log_rate[None] * LOG2E,
                               jnp.zeros((N_PAR - 9, n_width), jnp.float32)], axis=0)

        def now(step):
            return jnp.minimum(step, n_heads - 1)

        def late(step):
            return jnp.clip(step - LAG, 0, n_heads - 1)

        def blk_row(at):
            return pl.BlockSpec((n_batch, n_tok, block_w), lambda s: (0, 0, at(s)))

        tail_spec = pl.BlockSpec((n_batch, BLOCK, block_w), lambda s: (0, n_tok // BLOCK - 1, now(s + 1)))

        def mat_spec(at):
            return pl.BlockSpec((1, block_w, block_w), lambda s: (at(s), 0, 0))

        def par_spec(at):
            return pl.BlockSpec((N_PAR, block_w), lambda s: (0, at(s)))

        mask_spec = pl.BlockSpec((HALO + 1, n_tok, n_batch, LANES), lambda s: (0, 0, 0, 0), pipeline_mode=pl.Buffered(1))
        f32_slots = pltpu.VMEM((SLOTS, n_tok, n_batch, block_w), jnp.float32)
        f32_scr = pltpu.VMEM((n_tok, n_batch, block_w), jnp.float32)
        bf_scr = pltpu.VMEM((n_tok, n_batch, block_w), jnp.bfloat16)
        wire = pltpu.VMEM((n_heads, GROUP * PITCH, LANES), jnp.float32)
        half_wire = pltpu.VMEM((n_heads, GROUP * IN_ROWS, LANES), jnp.float32)
        sems = pltpu.SemaphoreType.DMA((n_heads,))

        item_f32 = functools.partial(pltpu.VMEM, dtype=jnp.float32)
        n_sems = 12
        du_time, grads = pl.pallas_call(
            functools.partial(fused_kernel, n_dev, n_heads), grid=(n_heads + LAG + AFTER[STAGES],),
            in_specs=[blk_row(now), tail_spec, blk_row(now), mask_spec, mat_spec(now), mat_spec(now),
                      mat_spec(late), mat_spec(late), par_spec(now), par_spec(late)],
            out_specs=[pl.BlockSpec(memory_space=pl.ANY)] * 2,
            out_shape=[jax.ShapeDtypeStruct((n_tok, n_batch, n_width), jnp.bfloat16),
                       jax.ShapeDtypeStruct((2, n_heads + 1, block_w, block_w), jnp.float32)],
            scratch_shapes=[pltpu.VMEM((SLOTS, n_tok + HALO, n_batch, block_w), jnp.float32)] + [f32_slots] * 7
            + [pltpu.VMEM((SLOTS, n_tok, n_batch, block_w), jnp.bfloat16), f32_scr, f32_scr, bf_scr, bf_scr] + [wire] * 2 + [half_wire] * 3
            + [item_f32((EDGE_SLOTS, HALO, n_batch, block_w))] * 2
            + [item_f32((PART_SLOTS, 2, block_w, block_w)), item_f32((FIRST_SLOTS, block_w, block_w)),
               item_f32((RECV_SLOTS, block_w // 2, block_w)), item_f32((RECV_SLOTS, block_w // 4, block_w)),
               item_f32((RECV_SLOTS, 3, block_w // 16, block_w)), item_f32((OWN_SLOTS, block_w, block_w)),
               item_f32((block_w, block_w)), item_f32((N_VEC, block_w)),
               pltpu.VMEM((EDGE_SLOTS, n_tok, n_batch, block_w), jnp.bfloat16)]
            + [item_f32((EDGE_SLOTS, HALO, n_batch, block_w))] * 2 + [item_f32((EDGE_IN, HALO, n_batch, block_w))]
            + [sems] * 2 + [pltpu.SemaphoreType.DMA((DEPTH - 1, n_heads))] * 2 + [sems] * 2 + [pltpu.SemaphoreType.DMA((EDGE_SLOTS,))] * 2
            + [pltpu.SemaphoreType.DMA((n_sems, OWN_SLOTS))] * 2
            + [pltpu.SemaphoreType.DMA((count,)) for count in (EDGE_SLOTS, EDGE_IN, EDGE_SLOTS, OWN_SLOTS)],
            compiler_params=pltpu.CompilerParams(vmem_limit_bytes=67043328, has_side_effects=True), name='fused_pass',
        )(u_in, u_in, grad_h, masks, a_gate_w, x_gate_w, a_gate_w, x_gate_w, par, par)
        vecs = grads[0, n_heads, :n_heads * N_VEC].reshape(n_heads, N_VEC, block_w)
        vecs = jnp.swapaxes(vecs, 0, 1).reshape(N_VEC, n_width)
        g_lam = 8.0 * jax.nn.sigmoid(-lam_param) * vecs[GLAM]
        return (jnp.swapaxes(du_time, 0, 1), vecs[GW:GW + CONV], vecs[GBC], grads[0, :n_heads], vecs[GBA],
                grads[1, :n_heads], vecs[GBI], g_lam)

    return jax.shard_map(local_fn, mesh=mesh,
                         in_specs=(seq_spec, P(None, 'cp'), seq_spec, rep_spec, rep_spec, rep_spec,
                                   rep_spec, rep_spec, rep_spec, rep_spec),
                         out_specs=(seq_spec,) + (rep_spec,) * 7, check_vma=False)
```

time: 281 us -> 224 us (0.80)
  Pallas kernels: 242 us -> 187 us
    pallas_call x1, Pallas kernels: 242 us -> 187 us  [local_fn(): pl.pallas_call(functools.partial(fused_kernel, n_dev, n_heads), grid=(n_h...]
    unnamed x16 -> x11, local copies, waits for them, and re-layouts: 11.2 us -> 11.1 us
where the time goes in v4:
time: 224 us
  Pallas kernels  187 us (83%)
  local copies, waits for them, and re-layouts  31.6 us (14%)
  starting transfers between devices  2.41 us (1%)
  other arithmetic  2.26 us (1%)
    pallas_call x1, Pallas kernels, local_fn(): pl.pallas_call(functools.partial(fused_kernel, n_dev, n_heads), grid=(n_h...  187 us
    unnamed x11, local copies, waits for them, and re-layouts  11.1 us
    squeeze x1, local copies, waits for them, and re-layouts, local_fn(): grads[1, :n_heads]  9.91 us
  transfers between devices with their start and end apart: 1, of which 0 were waited for; matrix products, arithmetic and copies ran while one was open for 2% of the time, Pallas kernels for 0%

profile of v4, /device:TPU:0, one launch (start us, length us, event | category | flops | bytes accessed | tf_op | source)
XLA Modules:
  0.0 224.0 jit_solution(9265181946426262499)
XLA Ops:
  0.6 0.8 slice.57
  1.4 2.4 %collective-permute-start = (s32[16,3]{1,0:T(8,128)S(1)}, s32[16,3]{1,0:T(8,128)S(1)}, u32[]{:S(2)}, u32[]{:S(2)}) collective-permute-start(s32[16,3]{1,0:T(8,128)S(1)} %slice.57), channel_id=1, source_target_pairs={{0,1},{1,2},{2,3},{3,4},{4,5},{5,6},{6,7},{7,8},{8,9},{9,10},{10,1... | collective-permute-start | bytes 584 | tf_op jit(solution)/shard_map/ppermute | solution.py:470
  3.8 0.1 fusion.7
  3.9 0.8 broadcast_in_dim.26
  4.7 0.8 broadcast_in_dim.27
  5.4 0.8 broadcast_in_dim.28
  6.2 0.8 broadcast_multiply_fusion
  7.0 2.4 %concatenate.7.par_ref.par2_ref = f32[16,5376]{1,0:T(8,128)} concatenate(f32[4,5376]{1,0:T(4,128)} %param.13, f32[1,5376]{1,0:T(1,128)S(1)} %broadcast_in_dim.26, f32[1,5376]{1,0:T(1,128)S(1)} %broadcast_in_dim.27, f32[1,5376]{1,0:T(1,128)S(1)} %broadcast_in_dim.28, f32[1,5376]{1,0:T(1,128)S(1)} %broadcast_in_dim.29, f32[1,5376]{1,0:T(1,128)S(1)} %mul.36, ...), dimensions={0} | concatenate | bytes 688128 | tf_op jit(solution)/shard_map/concatenate | solution.py:480
  9.4 0.0 collective-permute-done
  9.4 0.8 add_bitcast_fusion
  10.2 0.1 convert_bitcast_fusion.2
  10.3 0.1 copy.24
  10.4 1.9 broadcast_in_dim.12.mask_ref
  12.4 186.8 %fused_pass.1 = (bf16[64,16,5376]{2,1,0:T(8,128)(2,1)}, f32[2,22,256,256]{3,2,1,0:T(8,128)}) custom-call(bf16[16,64,5376]{2,1,0:T(8,128)(2,1)} %tail_ref.1, bf16[16,64,5376]{2,1,0:T(8,128)(2,1)} %tail_ref.1, f32[16,64,5376]{2,1,0:T(8,128)} %gh_ref.1, f32[4,64,16,128]{3,2,1,0:T(8,128)} %broadcast_in_dim.12.mask_ref, bf16[21,256,256]{2,1,0:T(8,128)(2,1)} %wa2_ref.1, ...), custom_call_target="tpu_custom_call" | custom-call | tf_op jit(solution)/shard_map/fused_pass/pallas_call | solution.py:510
  199.2 0.0 slice-start
  199.2 1.1 slice_bitcast_fusion.2
  200.3 0.0 slice-start.1
  200.3 0.0 slice-start.2
  200.3 9.9 %slice_bitcast_fusion = (f32[21,256,256]{2,1,0:T(8,128)}, f32[21,256,256]{2,1,0:T(8,128)}) fusion(f32[2,22,256,256]{3,2,1,0:T(8,128)} %get-tuple-element.11), kind=kLoop, calls=%fused_computation | loop fusion | bytes 22020096 | tf_op jit(solution)/shard_map/squeeze | solution.py:535
  210.2 0.1 copy.29
  210.3 0.0 slice-done
  210.3 0.0 slice-done.1
  210.4 0.0 slice-done.2
  210.4 0.0 copy-start
  210.4 10.4 %copy.26 = bf16[16,64,5376]{2,1,0:T(8,128)(2,1)} copy(bf16[16,64,5376]{2,0,1:T(8,128)(2,1)S(1)} %bitcast.25) | data formatting | bytes 22020096
  220.8 0.7 copy.27
  221.5 0.0 copy-done
  221.5 0.6 multiply_multiply_fusion
  222.1 0.6 squeeze.22
  222.7 0.6 squeeze.20
  223.3 0.6 squeeze.18
  (10 shorter events, 0.1 us)
Async XLA Ops:
  1.4 8.0 %collective-permute-start = (s32[16,3]{1,0:T(8,128)S(1)}, s32[16,3]{1,0:T(8,128)S(1)}, u32[]{:S(2)}, u32[]{:S(2)}) collective-permute-start(s32[16,3]{1,0:T(8,128)S(1)} %slice.57), channel_id=1, source_target_pairs={{0,1},{1,2},{2,3},{3,4},{4,5},{5,6},{6,7},{7,8},{8,9},{9,10},{10,1... | collective-permute-start | bytes 584 | tf_op jit(solution)/shard_map/ppermute | solution.py:470
  199.2 11.1 %slice-start = ((s8[11010048]{0:T(1024)(128)(4,1)}), s8[4194304]{0:T(1024)(128)(4,1)S(1)}, s32[]{:S(2)}) async-start(s8[11010048]{0:T(1024)(128)(4,1)} %bitcast.23), calls=%async_computation | async-start | bytes 8388608
  200.3 10.0 %slice-start.1 = ((s8[11010048]{0:T(1024)(128)(4,1)}), s8[4194304]{0:T(1024)(128)(4,1)S(1)}, s32[]{:S(2)}) async-start(s8[11010048]{0:T(1024)(128)(4,1)} %bitcast.23), calls=%async_computation.1 | async-start | bytes 8388608
  200.3 10.0 %slice-start.2 = ((s8[11010048]{0:T(1024)(128)(4,1)}), s8[2621440]{0:T(1024)(128)(4,1)S(1)}, s32[]{:S(2)}) async-start(s8[11010048]{0:T(1024)(128)(4,1)} %bitcast.23), calls=%async_computation.2 | async-start | bytes 5242880
  210.4 11.1 %copy-start = (f32[5376]{0:T(1024)S(1)}, f32[5376]{0:T(1024)}, u32[]{:S(2)}) copy-start(f32[5376]{0:T(1024)} %param.19) | copy-start | bytes 64516

commit v5 on v4

--- a/solution.py
+++ b/solution.py
@@ -62,11 +62,11 @@
 
 
 def fused_kernel(n_dev, n_heads,
-                 u_ref, tail_ref, gh_ref, mask_ref, wa_ref, wi_ref, wa2_ref, wi2_ref, par_ref, par2_ref,
+                 u_ref, tail_ref, gh_ref, seg_ref, wa_ref, wi_ref, wa2_ref, wi2_ref, par_ref, par2_ref,
                  du_ref, grad_ref,
                  u_s, c_s, r_s, i_s, a_s, m_s, e_s, g_s, cb_s, h_scr, d_scr, ga_scr, gi_scr,
-                 send, recv, group, resp, carry, halo_out, halo_in, part, got0, got1, got2, got3, own, vec_all, vec_ref, du_s, tail_s, edge_out, edge_in,
-                 send_sem, recv_sem, group_ssem, group_rsem, give_sem, take_sem, halo_ssem, halo_rsem, sum_ssem, sum_rsem, edge_ssem, edge_rsem, du_sem, put_sem):
+                 send, recv, group, resp, carry, halo_out, halo_in, mask_ref, seg_in, part, got0, got1, got2, got3, own, vec_all, vec_ref, du_s, tail_s, edge_out, edge_in,
+                 send_sem, recv_sem, group_ssem, group_rsem, give_sem, take_sem, halo_ssem, halo_rsem, seg_sem, sum_ssem, sum_rsem, edge_ssem, edge_rsem, du_sem, put_sem):
     n_batch, n_tok, width = u_ref.shape
     step_id = pl.program_id(0)
     me = lax.axis_index('cp')
@@ -195,7 +195,17 @@
     @pl.when(step_id == 0)
     def _begin():
         vec_all[...] = jnp.zeros_like(vec_all)
+        seg_copy = pltpu.make_async_remote_copy(src_ref=seg_ref.at[pl.ds(n_tok - HALO, HALO)], dst_ref=seg_in, send_sem=seg_sem.at[0],
+                                                recv_sem=seg_sem.at[1], device_id=(lax.rem(me + 1, n_dev),), device_id_type=MESH)
+        seg_copy.start()
         halo_send(0, u_ref)
+        seg_copy.wait_recv()
+        seg_copy.wait_send()
+        has_prev = jnp.where(me > 0, 1.0, 0.0)
+        for tap in range(1, CONV):
+            mask_ref[tap - 1, tap:] = jnp.where(seg_ref[tap:] == seg_ref[:n_tok - tap], 1.0, 0.0)
+            mask_ref[tap - 1, :tap] = jnp.where(seg_ref[:tap] == seg_in[HALO - tap:], 1.0, 0.0) * has_prev
+        mask_ref[HALO] = (1.0 - mask_ref[0]) * START_BIAS
 
     def group_copies(head):
         mine = group.at[head, block_of(z_at, PITCH, SUM_ROWS)]
@@ -459,23 +469,13 @@
 
 def solution(mesh):
     n_dev = mesh.shape['cp']
-    to_next = [(src, src + 1) for src in range(n_dev - 1)]
     seq_spec = P(None, 'cp', None)
     rep_spec = P()
 
     def local_fn(u_in, seg_ids, grad_h, conv_w, conv_b, a_gate_w, a_gate_b, x_gate_w, x_gate_b, lam_param):
         n_batch, n_tok, n_width = u_in.shape
         n_heads, block_w, _ = a_gate_w.shape
-        has_prev = lax.axis_index('cp') > 0
-        halo_seg = lax.ppermute(seg_ids[:, n_tok - HALO:], 'cp', to_next)
-        seg_ext = jnp.concatenate([halo_seg, seg_ids], axis=1).T
-        ext_ok = (jnp.arange(n_tok + HALO) >= HALO) | has_prev
-        masks = []
-        for tap in range(1, CONV):
-            tap_ok = (seg_ext[HALO - tap:HALO - tap + n_tok] == seg_ext[HALO:]) & ext_ok[HALO - tap:HALO - tap + n_tok, None]
-            masks.append(tap_ok.astype(jnp.float32))
-        masks.append((1.0 - masks[0]) * START_BIAS)
-        masks = jnp.broadcast_to(jnp.stack(masks)[..., None], (HALO + 1, n_tok, n_batch, LANES))
+        seg_time = jnp.broadcast_to(seg_ids.T[:, :, None], (n_tok, n_batch, LANES))
         log_rate = -8.0 * jax.nn.softplus(-lam_param)
         par = jnp.concatenate([conv_w, conv_b[None], a_gate_b[None], x_gate_b[None], log_rate[None], log_rate[None] * LOG2E,
                                jnp.zeros((N_PAR - 9, n_width), jnp.float32)], axis=0)
@@ -497,7 +497,7 @@
         def par_spec(at):
             return pl.BlockSpec((N_PAR, block_w), lambda s: (0, at(s)))
 
-        mask_spec = pl.BlockSpec((HALO + 1, n_tok, n_batch, LANES), lambda s: (0, 0, 0, 0), pipeline_mode=pl.Buffered(1))
+        seg_spec = pl.BlockSpec((n_tok, n_batch, LANES), lambda s: (0, 0, 0), pipeline_mode=pl.Buffered(1))
         f32_slots = pltpu.VMEM((SLOTS, n_tok, n_batch, block_w), jnp.float32)
         f32_scr = pltpu.VMEM((n_tok, n_batch, block_w), jnp.float32)
         bf_scr = pltpu.VMEM((n_tok, n_batch, block_w), jnp.bfloat16)
@@ -509,7 +509,7 @@
         n_sems = 12
         du_time, grads = pl.pallas_call(
             functools.partial(fused_kernel, n_dev, n_heads), grid=(n_heads + LAG + AFTER[STAGES],),
-            in_specs=[blk_row(now), tail_spec, blk_row(now), mask_spec, mat_spec(now), mat_spec(now),
+            in_specs=[blk_row(now), tail_spec, blk_row(now), seg_spec, mat_spec(now), mat_spec(now),
                       mat_spec(late), mat_spec(late), par_spec(now), par_spec(late)],
             out_specs=[pl.BlockSpec(memory_space=pl.ANY)] * 2,
             out_shape=[jax.ShapeDtypeStruct((n_tok, n_batch, n_width), jnp.bfloat16),
@@ -517,6 +517,7 @@
             scratch_shapes=[pltpu.VMEM((SLOTS, n_tok + HALO, n_batch, block_w), jnp.float32)] + [f32_slots] * 7
             + [pltpu.VMEM((SLOTS, n_tok, n_batch, block_w), jnp.bfloat16), f32_scr, f32_scr, bf_scr, bf_scr] + [wire] * 2 + [half_wire] * 3
             + [item_f32((EDGE_SLOTS, HALO, n_batch, block_w))] * 2
+            + [item_f32((HALO + 1, n_tok, n_batch, LANES)), pltpu.VMEM((HALO, n_batch, LANES), jnp.int32)]
             + [item_f32((PART_SLOTS, 2, block_w, block_w)), item_f32((FIRST_SLOTS, block_w, block_w)),
                item_f32((RECV_SLOTS, block_w // 2, block_w)), item_f32((RECV_SLOTS, block_w // 4, block_w)),
                item_f32((RECV_SLOTS, 3, block_w // 16, block_w)), item_f32((OWN_SLOTS, block_w, block_w)),
@@ -524,10 +525,11 @@
                pltpu.VMEM((EDGE_SLOTS, n_tok, n_batch, block_w), jnp.bfloat16)]
             + [item_f32((EDGE_SLOTS, HALO, n_batch, block_w))] * 2 + [item_f32((EDGE_IN, HALO, n_batch, block_w))]
             + [sems] * 2 + [pltpu.SemaphoreType.DMA((DEPTH - 1, n_heads))] * 2 + [sems] * 2 + [pltpu.SemaphoreType.DMA((EDGE_SLOTS,))] * 2
+            + [pltpu.SemaphoreType.DMA((2,))]
             + [pltpu.SemaphoreType.DMA((n_sems, OWN_SLOTS))] * 2
             + [pltpu.SemaphoreType.DMA((count,)) for count in (EDGE_SLOTS, EDGE_IN, EDGE_SLOTS, OWN_SLOTS)],
             compiler_params=pltpu.CompilerParams(vmem_limit_bytes=67043328, has_side_effects=True), name='fused_pass',
-        )(u_in, u_in, grad_h, masks, a_gate_w, x_gate_w, a_gate_w, x_gate_w, par, par)
+        )(u_in, u_in, grad_h, seg_time, a_gate_w, x_gate_w, a_gate_w, x_gate_w, par, par)
         vecs = grads[0, n_heads, :n_heads * N_VEC].reshape(n_heads, N_VEC, block_w)
         vecs = jnp.swapaxes(vecs, 0, 1).reshape(N_VEC, n_width)
         g_lam = 8.0 * jax.nn.sigmoid(-lam_param) * vecs[GLAM]

time: 224 us -> 218 us (0.973)
  local copies, waits for them, and re-layouts: 31.6 us -> 26.8 us
  starting transfers between devices: 2.41 us -> 0 us
    squeeze x1, local copies, waits for them, and re-layouts: 9.91 us -> 5.47 us  [local_fn(): grads[1, :n_heads]]
    ppermute x1 -> x0, starting transfers between devices: 2.41 us -> none  [local_fn(): halo_seg = lax.ppermute(seg_ids[:, n_tok - HALO:], 'cp', to_next)]
    unnamed x11 -> x7, local copies, waits for them, and re-layouts: 11.1 us -> 12.9 us
  transfers between devices with their start and end apart: 1 -> 0, of which waited for: 0 -> 0; matrix products, arithmetic and copies ran while one was open for 2% -> 0% of each run, Pallas kernels for 0% -> 0%
where the time goes in v5:
time: 218 us
  Pallas kernels  189 us (87%)
  local copies, waits for them, and re-layouts  26.8 us (12%)
    pallas_call x1, Pallas kernels, local_fn(): pl.pallas_call(functools.partial(fused_kernel, n_dev, n_heads), grid=(n_h...  189 us
    unnamed x7, local copies, waits for them, and re-layouts  12.9 us
    squeeze x1, local copies, waits for them, and re-layouts, local_fn(): grads[1, :n_heads]  5.47 us

profile of v5, /device:TPU:0, one launch (start us, length us, event | category | flops | bytes accessed | tf_op | source)
XLA Modules:
  0.0 217.6 jit_solution(12235521279140653412)
XLA Ops:
  0.6 0.8 broadcast_in_dim.23
  1.4 0.8 broadcast_in_dim.24
  2.1 0.8 broadcast_in_dim.25
  2.9 0.8 copy.24
  3.7 0.8 broadcast_multiply_fusion
  4.5 2.4 %concatenate.3.par_ref.par2_ref = f32[16,5376]{1,0:T(8,128)} concatenate(f32[4,5376]{1,0:T(4,128)} %param.13, f32[1,5376]{1,0:T(1,128)S(1)} %broadcast_in_dim.23, f32[1,5376]{1,0:T(1,128)S(1)} %broadcast_in_dim.24, f32[1,5376]{1,0:T(1,128)S(1)} %broadcast_in_dim.25, f32[1,5376]{1,0:T(1,128)S(1)} %broadcast_in_dim.26, f32[1,5376]{1,0:T(1,128)S(1)} %mul.28, ...), dimensions={0} | concatenate | bytes 688128 | tf_op jit(solution)/shard_map/concatenate | solution.py:480
  6.9 1.0 broadcast_in_dim.22.seg_ref
  7.9 188.7 %fused_pass.1 = (bf16[64,16,5376]{2,1,0:T(8,128)(2,1)}, f32[2,22,256,256]{3,2,1,0:T(8,128)}) custom-call(bf16[16,64,5376]{2,1,0:T(8,128)(2,1)} %tail_ref.1, bf16[16,64,5376]{2,1,0:T(8,128)(2,1)} %tail_ref.1, f32[16,64,5376]{2,1,0:T(8,128)} %gh_ref.1, s32[64,16,128]{2,1,0:T(8,128)} %broadcast_in_dim.22.seg_ref, bf16[21,256,256]{2,1,0:T(8,128)(2,1)} %wa2_ref.1, ...), custom_call_target="tpu_custom_call" | custom-call | tf_op jit(solution)/shard_map/fused_pass/pallas_call | solution.py:510
  196.7 0.0 copy-start
  196.7 12.2 %copy.26 = bf16[16,64,5376]{2,1,0:T(8,128)(2,1)} copy(bf16[16,64,5376]{2,0,1:T(8,128)(2,1)} %bitcast.14) | data formatting | bytes 22020096
  208.9 0.0 copy-done
  208.9 0.0 copy-start.1
  208.9 5.5 %slice_bitcast_fusion = (f32[21,256,256]{2,1,0:T(8,128)}, f32[21,256,256]{2,1,0:T(8,128)}) fusion(f32[2,22,256,256]{3,2,1,0:T(8,128)S(1)} %copy-done), kind=kLoop, calls=%fused_computation | loop fusion | bytes 22020096 | tf_op jit(solution)/shard_map/squeeze | solution.py:537
  214.4 0.1 copy.29
  214.5 0.7 copy.27
  215.1 0.0 copy-done.1
  215.1 0.6 multiply_multiply_fusion
  215.8 0.6 squeeze.22
  216.4 0.6 squeeze.20
  217.0 0.6 squeeze.18
  (7 shorter events, 0.1 us)
Async XLA Ops:
  196.7 12.2 %copy-start = (f32[2,22,256,256]{3,2,1,0:T(8,128)S(1)}, f32[2,22,256,256]{3,2,1,0:T(8,128)}, u32[]{:S(2)}) copy-start(f32[2,22,256,256]{3,2,1,0:T(8,128)} %get-tuple-element.11) | copy-start | bytes 34603012
  208.9 6.3 %copy-start.1 = (f32[5376]{0:T(1024)S(1)}, f32[5376]{0:T(1024)}, u32[]{:S(2)}) copy-start(f32[5376]{0:T(1024)} %param.19) | copy-start | bytes 64516

commit v6 on v5

--- a/solution.py
+++ b/solution.py
@@ -26,7 +26,7 @@
 MESH = pl.DeviceIdType.MESH
 
 W0, BC, BA, BI, KL, KE = 0, 4, 5, 6, 7, 8
-N_PAR = 16
+N_PAR = 9
 GW, GBC, GBA, GBI, GLAM = 0, 4, 5, 6, 7
 N_VEC = 8
 
@@ -477,8 +477,7 @@
         n_heads, block_w, _ = a_gate_w.shape
         seg_time = jnp.broadcast_to(seg_ids.T[:, :, None], (n_tok, n_batch, LANES))
         log_rate = -8.0 * jax.nn.softplus(-lam_param)
-        par = jnp.concatenate([conv_w, conv_b[None], a_gate_b[None], x_gate_b[None], log_rate[None], log_rate[None] * LOG2E,
-                               jnp.zeros((N_PAR - 9, n_width), jnp.float32)], axis=0)
+        par = jnp.concatenate([conv_w, conv_b[None], a_gate_b[None], x_gate_b[None], log_rate[None], log_rate[None] * LOG2E], axis=0)
 
         def now(step):
             return jnp.minimum(step, n_heads - 1)

time: 218 us -> 218 us (level)
  no operation moved by 1% of the time
where the time goes in v6:
time: 218 us
  Pallas kernels  189 us (87%)
  local copies, waits for them, and re-layouts  26.7 us (12%)
    pallas_call x1, Pallas kernels, local_fn(): pl.pallas_call(functools.partial(fused_kernel, n_dev, n_heads), grid=(n_h...  189 us
    unnamed x7, local copies, waits for them, and re-layouts  12.9 us
    squeeze x1, local copies, waits for them, and re-layouts, local_fn(): grads[1, :n_heads]  5.47 us

profile of v6, /device:TPU:0, one launch (start us, length us, event | category | flops | bytes accessed | tf_op | source)
XLA Modules:
  0.0 217.7 jit_solution(2410817185841549807)
XLA Ops:
  0.6 0.8 broadcast_in_dim.20
  1.4 0.8 broadcast_in_dim.21
  2.1 0.8 broadcast_in_dim.22
  2.9 0.8 copy.24
  3.7 0.8 broadcast_multiply_fusion
  4.5 2.4 %concatenate.3.par_ref.par2_ref = f32[9,5376]{1,0:T(8,128)} concatenate(f32[4,5376]{1,0:T(4,128)} %param.13, f32[1,5376]{1,0:T(1,128)S(1)} %broadcast_in_dim.20, f32[1,5376]{1,0:T(1,128)S(1)} %broadcast_in_dim.21, f32[1,5376]{1,0:T(1,128)S(1)} %broadcast_in_dim.22, f32[1,5376]{1,0:T(1,128)S(1)} %broadcast_in_dim.23, f32[1,5376]{1,0:T(1,128)S(1)} %mul.28), dimensions={0} | concatenate | bytes 387072 | tf_op jit(solution)/shard_map/concatenate | solution.py:480
  6.9 1.0 broadcast_in_dim.19.seg_ref
  7.9 188.8 %fused_pass.1 = (bf16[64,16,5376]{2,1,0:T(8,128)(2,1)}, f32[2,22,256,256]{3,2,1,0:T(8,128)}) custom-call(bf16[16,64,5376]{2,1,0:T(8,128)(2,1)} %tail_ref.1, bf16[16,64,5376]{2,1,0:T(8,128)(2,1)} %tail_ref.1, f32[16,64,5376]{2,1,0:T(8,128)} %gh_ref.1, s32[64,16,128]{2,1,0:T(8,128)} %broadcast_in_dim.19.seg_ref, bf16[21,256,256]{2,1,0:T(8,128)(2,1)} %wa2_ref.1, ...), custom_call_target="tpu_custom_call" | custom-call | tf_op jit(solution)/shard_map/fused_pass/pallas_call | solution.py:509
  196.7 0.0 copy-start
  196.7 12.2 %copy.26 = bf16[16,64,5376]{2,1,0:T(8,128)(2,1)} copy(bf16[16,64,5376]{2,0,1:T(8,128)(2,1)} %bitcast.14) | data formatting | bytes 22020096
  208.9 0.0 copy-done
  208.9 0.0 copy-start.1
  209.0 5.5 %slice_bitcast_fusion = (f32[21,256,256]{2,1,0:T(8,128)}, f32[21,256,256]{2,1,0:T(8,128)}) fusion(f32[2,22,256,256]{3,2,1,0:T(8,128)S(1)} %copy-done), kind=kLoop, calls=%fused_computation | loop fusion | bytes 22020096 | tf_op jit(solution)/shard_map/squeeze | solution.py:536
  214.4 0.1 copy.29
  214.5 0.7 copy.27
  215.2 0.0 copy-done.1
  215.2 0.6 multiply_multiply_fusion
  215.8 0.6 squeeze.22
  216.4 0.6 squeeze.20
  217.0 0.6 squeeze.18
  (6 shorter events, 0.1 us)
Async XLA Ops:
  196.7 12.2 %copy-start = (f32[2,22,256,256]{3,2,1,0:T(8,128)S(1)}, f32[2,22,256,256]{3,2,1,0:T(8,128)}, u32[]{:S(2)}) copy-start(f32[2,22,256,256]{3,2,1,0:T(8,128)} %get-tuple-element.11) | copy-start | bytes 34603012
  208.9 6.3 %copy-start.1 = (f32[5376]{0:T(1024)S(1)}, f32[5376]{0:T(1024)}, u32[]{:S(2)}) copy-start(f32[5376]{0:T(1024)} %param.19) | copy-start | bytes 64516
